TPU v7x, 32 devices: a whole 2x2x4 slice. The times are simulated.
32 devices in a mesh: rep: 1, dp: 32 (over x, y, z, core).
Axes of the slice: x: 2, y: 2, z: 4, core: 2. Of those that a mesh axis runs over, the one named last changes fastest.
Arguments:
- x: bfloat16 [32, 2048, 1024], P(('rep', 'dp'))
- dy: bfloat16 [32, 2048, 1024], P(('rep', 'dp'))
- w_gate: bfloat16 [2, 1024, 2816], P(None, 'dp')
- w_up: bfloat16 [2, 1024, 2816], P(None, 'dp')
- w_down: bfloat16 [2, 2816, 1024], P(None, 'dp')
- m_w_gate: float32 [2, 1024, 2816], P(None, 'dp')
- m_w_up: float32 [2, 1024, 2816], P(None, 'dp')
- m_w_down: float32 [2, 2816, 1024], P(None, 'dp')
- v_w_gate: float32 [2, 1024, 2816], P(None, 'dp')
- v_w_up: float32 [2, 1024, 2816], P(None, 'dp')
- v_w_down: float32 [2, 2816, 1024], P(None, 'dp')
Outputs:
- output 1: bfloat16 [2, 1024, 2816], P('rep', 'dp')
- output 2: bfloat16 [2, 1024, 2816], P('rep', 'dp')
- output 3: bfloat16 [2, 2816, 1024], P('rep', 'dp')
- output 4: float32 [2, 1024, 2816], P('rep', 'dp')
- output 5: float32 [2, 1024, 2816], P('rep', 'dp')
- output 6: float32 [2, 2816, 1024], P('rep', 'dp')
- output 7: float32 [2, 1024, 2816], P('rep', 'dp')
- output 8: float32 [2, 1024, 2816], P('rep', 'dp')
- output 9: float32 [2, 2816, 1024], P('rep', 'dp')
All inputs are finite; a program needn't handle non-finite values.
Results may differ from a plain program's by a relative error of at most 0.0279.
Values are sent between devices in bfloat16 or wider.
A program may use at most 2 GiB of HBM per device.

v0:
```python
import jax
import jax.numpy as jnp
from jax import lax
from jax.sharding import PartitionSpec as P

NAMES = ("w_gate", "w_up", "w_down")


def matmul(a, w):
    return jnp.dot(a, w, preferred_element_type=jnp.float32).astype(jnp.bfloat16)


def normed(h):
    wide = h.astype(jnp.float32)
    scale = lax.rsqrt(jnp.mean(wide**2, -1, keepdims=True) + 1e-6)
    return (wide * scale).astype(jnp.bfloat16)


def layer(h, w):
    a = normed(h)
    gate = jnp.dot(a, w["w_gate"], preferred_element_type=jnp.float32)
    up = jnp.dot(a, w["w_up"], preferred_element_type=jnp.float32)
    return h + matmul((jax.nn.silu(gate) * up).astype(jnp.bfloat16), w["w_down"])


def adamw(w, m, v, g):
    m = 0.9 * m + 0.1 * g
    v = 0.95 * v + 0.05 * g * g
    step = m * lax.rsqrt(v + 1e-8) + 0.1 * w
    return (w - 0.02 * step).astype(jnp.bfloat16), m, v


def clipped(gradients, sum_of_squares, count):
    factor = jnp.minimum(1.0, 0.5 * lax.rsqrt(sum_of_squares / count + 1e-30))
    return [g * factor for g in gradients]


def solution(mesh):
    def fetched(weights, number):
        return {name: lax.all_gather(w[number], "dp", axis=0, tiled=True) for name, w in zip(NAMES, weights, strict=True)}

    def step(x, dy, *arrays):
        weights, m, v = (arrays[i : i + 3] for i in (0, 3, 6))
        layers = weights[0].shape[0]
        h, kept = x[0], []
        for number in range(layers):
            kept.append(h)
            h = layer(h, fetched(weights, number))
        by_h, mine = dy[0], [None] * layers
        for number in reversed(range(layers)):
            _, back = jax.vjp(lambda w, h: layer(h, w), fetched(weights, number), kept[number])
            by_w, by_h = back(by_h)
            mine[number] = [lax.psum_scatter(by_w[name], "dp", scatter_dimension=0, tiled=True) for name in NAMES]
        gradients = [jnp.stack([mine[number][i] for number in range(layers)]).astype(jnp.float32) for i in range(3)]
        squares = lax.psum(sum(jnp.sum(g * g) for g in gradients), "dp")
        gradients = clipped(gradients, squares, lax.psum(1, "dp") * sum(g.size for g in gradients))
        new = [adamw(w.astype(jnp.float32), m, v, g) for w, m, v, g in zip(weights, m, v, gradients, strict=True)]
        return tuple(one[which] for which in range(3) for one in new)

    states, cut = P(("rep", "dp"), None, None), P(None, "dp", None)
    return jax.shard_map(
        step,
        mesh=mesh,
        in_specs=(states, states) + (cut,) * 9,
        out_specs=(P("rep", "dp", None),) * 9,
        check_vma=False,
    )
```

profile of v0, /device:TPU:0, one launch (start us, length us, event | category | flops | bytes accessed | tf_op | source)
XLA Modules:
  0.0 1452.8 jit_solution(11529697896116047488)
XLA Ops:
  7.2 1.8 fusion.94
  9.0 0.0 all-gather.15.cloned.1.call-start
  9.1 1.8 fusion.93
  10.8 0.0 all-gather.17.cloned.1.call-start
  10.9 1.8 fusion.92
  12.7 0.5 all-gather.21.cloned.1.call-update
  13.3 0.5 all-gather.23.cloned.1.call-update
  13.9 0.5 all-gather.19.cloned.1.call-update
  14.5 6.5 copy.20
  21.0 3.1 fusion.15
  24.1 6.6 copy.21
  30.6 51.3 %all-gather.13.cloned.1.call-done = bf16[1,1024,2816]{2,1,0:T(8,128)(2,1)} async-done(((bf16[1,32,2816]{2,1,0:T(8,128)(2,1)}), bf16[1,1024,2816]{2,1,0:T(8,128)(2,1)}) %all-gather.13.cloned.1.call-update) | async-done | bytes 5767184 | tf_op jit(solution)/shard_map/all_gather | solution.py:40
  82.0 20.0 %fusion.35 = f32[2048,2816]{1,0:T(8,128)} fusion(bf16[1,1024,2816]{2,1,0:T(8,128)(2,1)} %all-gather.13.cloned.1.call-done, bf16[1,2048,1024]{1,2,0:T(8,128)(2,1)} %copy.20, f32[2048]{0:T(1024)S(1)} %add_rsqrt_fusion), kind=kOutput, calls=%fused_computation.53 | convolution fusion | flops 11817451520 | bytes 33038336 | tf_op jit(solution)/shard_map/dot_general | solution.py:21
  101.9 49.6 %all-gather.15.cloned.1.call-done = bf16[1,1024,2816]{2,1,0:T(8,128)(2,1)} async-done(((bf16[1,32,2816]{2,1,0:T(8,128)(2,1)}), bf16[1,1024,2816]{2,1,0:T(8,128)(2,1)}) %all-gather.15.cloned.1.call-update) | async-done | bytes 5767184 | tf_op jit(solution)/shard_map/all_gather | solution.py:40
  151.5 27.8 %multiply_convert_fusion.1 = (bf16[2048,2816]{1,0:T(8,128)(2,1)}, f32[2048,2816]{1,0:T(8,128)}) fusion(f32[2048,2816]{1,0:T(8,128)} %fusion.35, bf16[1,1024,2816]{2,1,0:T(8,128)(2,1)} %all-gather.15.cloned.1.call-done, bf16[1,2048,1024]{1,2,0:T(8,128)(2,1)} %copy.20, f32[2048]{0:T(1024)S(1)} %add_rsqrt_fusion), kind=kOutput, calls=%fused_computation.17 | convolution fusion | flops 11852054528 | bytes 67641344 | tf_op jit(solution)/shard_map/dot_general | solution.py:22
  179.3 41.8 %all-gather.17.cloned.1.call-done = bf16[1,2816,1024]{2,1,0:T(8,128)(2,1)} async-done(((bf16[1,88,1024]{2,1,0:T(8,128)(2,1)}), bf16[1,2816,1024]{2,1,0:T(8,128)(2,1)}) %all-gather.17.cloned.1.call-update) | async-done | bytes 5767184 | tf_op jit(solution)/shard_map/all_gather | solution.py:40
  221.1 19.8 %fusion.19 = (f32[2048]{0:T(1024)S(1)}, bf16[2048,1024]{0,1:T(8,128)(2,1)}) fusion(bf16[2048,2816]{1,0:T(8,128)(2,1)} %get-tuple-element.24, bf16[1,2816,1024]{2,1,0:T(8,128)(2,1)} %all-gather.17.cloned.1.call-done, bf16[1,2048,1024]{1,2,0:T(8,128)(2,1)} %copy.20), kind=kOutput, calls=%fused_computation.37 | convolution fusion | flops 11821643776 | bytes 25698304 | tf_op jit(solution)/shard_map/dot_general | solution.py:10
  240.9 49.6 %all-gather.21.cloned.1.call-done = bf16[1,2816,1024]{2,1,0:T(8,128)(2,1)} async-done(((bf16[1,88,1024]{2,1,0:T(8,128)(2,1)}), bf16[1,2816,1024]{2,1,0:T(8,128)(2,1)}) %all-gather.21.cloned.1.call-update) | async-done | bytes 5767184 | tf_op jit(solution)/shard_map/all_gather | solution.py:40
  290.6 18.2 %convolution_convert_fusion.1 = bf16[2048,2816]{1,0:T(8,128)(2,1)} fusion(bf16[1,2816,1024]{2,1,0:T(8,128)(2,1)} %all-gather.21.cloned.1.call-done, bf16[1,2048,1024]{2,1,0:T(8,128)(2,1)} %param.12), kind=kOutput, calls=%fused_computation.29 | convolution fusion | flops 11816927232 | bytes 21495808 | tf_op jit(solution)/shard_map/transpose(jvp())/dot_general | solution.py:10
  308.7 51.3 %all-gather.23.cloned.1.call-done = bf16[1,1024,2816]{2,1,0:T(8,128)(2,1)} async-done(((bf16[1,32,2816]{2,1,0:T(8,128)(2,1)}), bf16[1,1024,2816]{2,1,0:T(8,128)(2,1)}) %all-gather.23.cloned.1.call-update) | async-done | bytes 5767184 | tf_op jit(solution)/shard_map/all_gather | solution.py:40
  360.0 20.1 %fusion.22 = f32[2048,2816]{1,0:T(8,128)} fusion(bf16[1,1024,2816]{2,1,0:T(8,128)(2,1)} %all-gather.23.cloned.1.call-done, bf16[2048,1024]{0,1:T(8,128)(2,1)} %get-tuple-element.27, f32[2048]{0:T(1024)S(1)} %fusion.80), kind=kOutput, calls=%fused_computation.40 | convolution fusion | flops 11817451520 | bytes 33038336 | tf_op jit(solution)/shard_map/jvp()/dot_general | solution.py:22
  380.1 49.4 %all-gather.19.cloned.1.call-done = bf16[1,1024,2816]{2,1,0:T(8,128)(2,1)} async-done(((bf16[1,32,2816]{2,1,0:T(8,128)(2,1)}), bf16[1,1024,2816]{2,1,0:T(8,128)(2,1)}) %all-gather.19.cloned.1.call-update) | async-done | bytes 5767184 | tf_op jit(solution)/shard_map/all_gather | solution.py:40
  429.4 34.4 %fusion.2 = (bf16[2048,2816]{1,0:T(8,128)(2,1)}, f32[2048,2816]{1,0:T(8,128)}) fusion(f32[2048,2816]{1,0:T(8,128)} %fusion.22, bf16[2048,2816]{1,0:T(8,128)(2,1)} %convolution_convert_fusion.1, bf16[1,1024,2816]{2,1,0:T(8,128)(2,1)} %all-gather.19.cloned.1.call-done, bf16[2048,1024]{0,1:T(8,128)(2,1)} %get-tuple-element.27, f32[2048]{0:T(1024)S(1)} %fusion.80), kind=kOutput, calls=%fused_computation.8 | convolution fusion | flops 11886657536 | bytes 79175680 | tf_op jit(solution)/shard_map/jvp()/dot_general | solution.py:21
  463.8 21.7 %fusion.12 = bf16[2048,1024]{0,1:T(8,128)(2,1)} fusion(bf16[2048,2816]{1,0:T(8,128)(2,1)} %convolution_convert_fusion.1, bf16[1,1024,2816]{2,1,0:T(8,128)(2,1)} %all-gather.23.cloned.1.call-done, f32[2048,2816]{1,0:T(8,128)} %get-tuple-element.29), kind=kOutput, calls=%fused_computation.21 | convolution fusion | flops 11845763072 | bytes 44564480 | tf_op jit(solution)/shard_map/transpose(jvp())/dot_general | solution.py:22
  485.5 18.9 %fusion.21 = (f32[2048]{0:T(1024)S(1)}, bf16[2048,1024]{0,1:T(8,128)(2,1)S(1)}) fusion(bf16[2048,1024]{0,1:T(8,128)(2,1)} %get-tuple-element.27, bf16[2048,1024]{0,1:T(8,128)(2,1)} %fusion.12, bf16[2048,2816]{1,0:T(8,128)(2,1)} %get-tuple-element.28, bf16[1,1024,2816]{2,1,0:T(8,128)(2,1)} %all-gather.19.cloned.1.call-done), kind=kOutput, calls=%fused_computation.39 | convolution fusion | flops 11821643776 | bytes 29892608 | tf_op jit(solution)/shard_map/transpose(jvp())/dot_general | solution.py:21
  504.4 3.6 fusion.43
  508.0 2.0 copy-done.2
  510.0 17.2 %convolution_convert_fusion.2 = bf16[2816,1024]{1,0:T(8,128)(2,1)} fusion(bf16[2048,2816]{1,0:T(8,128)(2,1)} %get-tuple-element.24, bf16[2048,1024]{0,1:T(8,128)(2,1)S(1)} %fusion.43), kind=kOutput, calls=%fused_computation.59 | convolution fusion | flops 11814043648 | bytes 21495808 | tf_op jit(solution)/shard_map/transpose(jvp())/dot_general | solution.py:10
  527.2 0.0 reduce-scatter.17.cloned.1.call-start
  527.3 23.5 %fusion.37 = bf16[2816,1024]{1,0:T(8,128)(2,1)} fusion(f32[2048,2816]{1,0:T(8,128)} %fusion.22, bf16[1,2048,1024]{2,1,0:T(8,128)(2,1)} %param.12, f32[2048,2816]{1,0:T(8,128)} %get-tuple-element.29), kind=kOutput, calls=%fused_computation.55 | convolution fusion | flops 11848646656 | bytes 56098816 | tf_op jit(solution)/shard_map/transpose(jvp())/dot_general | solution.py:10
  550.9 18.5 %convolution_convert_fusion = bf16[2048,2816]{1,0:T(8,128)(2,1)} fusion(bf16[2048,1024]{0,1:T(8,128)(2,1)} %copy-done.2, bf16[1,2816,1024]{2,1,0:T(8,128)(2,1)} %all-gather.17.cloned.1.call-done), kind=kOutput, calls=%fused_computation.28 | convolution fusion | flops 11816927232 | bytes 21495808 | tf_op jit(solution)/shard_map/transpose(jvp())/dot_general | solution.py:10
  569.4 22.5 %fusion.42 = bf16[1024,2816]{1,0:T(8,128)(2,1)} fusion(bf16[2048,2816]{1,0:T(8,128)(2,1)} %convolution_convert_fusion, f32[2048,2816]{1,0:T(8,128)} %fusion.35, bf16[1,2048,1024]{1,2,0:T(8,128)(2,1)} %copy.20, f32[2048]{0:T(1024)S(1)} %copy-done.14), kind=kOutput, calls=%fused_computation.58 | convolution fusion | flops 11854938112 | bytes 44572672 | tf_op jit(solution)/shard_map/transpose(jvp())/dot_general | solution.py:22
  592.0 22.7 %fusion.38 = bf16[1024,2816]{1,0:T(8,128)(2,1)} fusion(bf16[2048,2816]{1,0:T(8,128)(2,1)} %convolution_convert_fusion.1, bf16[2048,1024]{0,1:T(8,128)(2,1)} %get-tuple-element.27, f32[2048]{0:T(1024)S(1)} %copy-done.10, f32[2048,2816]{1,0:T(8,128)} %get-tuple-element.29), kind=kOutput, calls=%fused_computation.56 | convolution fusion | flops 11854938112 | bytes 44572672 | tf_op jit(solution)/shard_map/transpose(jvp())/dot_general | solution.py:22
  614.7 0.0 reduce-scatter.7.cloned.1.call-start
  614.8 27.0 %fusion.39 = bf16[1024,2816]{1,0:T(8,128)(2,1)} fusion(f32[2048,2816]{1,0:T(8,128)} %fusion.35, f32[2048,2816]{1,0:T(8,128)} %get-tuple-element.25, bf16[2048,2816]{1,0:T(8,128)(2,1)} %convolution_convert_fusion, bf16[1,2048,1024]{1,2,0:T(8,128)(2,1)} %copy.20, f32[2048]{0:T(1024)S(1)} %copy-done.14), kind=kOutput, calls=%fused_computation.57 | convolution fusion | flops 11883773952 | bytes 67641344 | tf_op jit(solution)/shard_map/transpose(jvp())/dot_general | solution.py:21
  641.9 19.0 %convolution_convert_fusion.3 = bf16[1024,2816]{1,0:T(8,128)(2,1)} fusion(bf16[2048,2816]{1,0:T(8,128)(2,1)} %get-tuple-element.28, bf16[2048,1024]{0,1:T(8,128)(2,1)} %get-tuple-element.27, f32[2048]{0:T(1024)S(1)} %copy-done.10), kind=kOutput, calls=%fused_computation.60 | convolution fusion | flops 11817451520 | bytes 21504000 | tf_op jit(solution)/shard_map/transpose(jvp())/dot_general | solution.py:21
  661.0 10.5 reduce-scatter.15.cloned.1.call-done
  671.5 145.2 %reduce-scatter.17.cloned.1.call-done = bf16[88,1024]{1,0:T(8,128)(2,1)} async-done(((bf16[2816,1024]{1,0:T(8,128)(2,1)}), bf16[88,1024]{1,0:T(8,128)(2,1)}) %reduce-scatter.17.cloned.1.call-update) | async-done | bytes 180240 | tf_op jit(solution)/shard_map/reduce_scatter | solution.py:53
  816.6 1.8 fusion.70
  818.4 143.6 %reduce-scatter.11.cloned.1.call-done = bf16[32,2816]{1,0:T(8,128)(2,1)} async-done(((bf16[1024,2816]{1,0:T(8,128)(2,1)}), bf16[32,2816]{1,0:T(8,128)(2,1)}) %reduce-scatter.11.cloned.1.call-update) | async-done | bytes 180240 | tf_op jit(solution)/shard_map/reduce_scatter | solution.py:53
  962.0 145.2 %reduce-scatter.13.cloned.1.call-done = bf16[32,2816]{1,0:T(8,128)(2,1)} async-done(((bf16[1024,2816]{1,0:T(8,128)(2,1)}), bf16[32,2816]{1,0:T(8,128)(2,1)}) %reduce-scatter.13.cloned.1.call-update) | async-done | bytes 180240 | tf_op jit(solution)/shard_map/reduce_scatter | solution.py:53
  1107.2 1.8 fusion.69
  1109.0 143.6 %reduce-scatter.7.cloned.1.call-done = bf16[32,2816]{1,0:T(8,128)(2,1)} async-done(((bf16[1024,2816]{1,0:T(8,128)(2,1)}), bf16[32,2816]{1,0:T(8,128)(2,1)}) %reduce-scatter.7.cloned.1.call-update) | async-done | bytes 180240 | tf_op jit(solution)/shard_map/reduce_scatter | solution.py:53
  1252.6 145.2 %reduce-scatter.9.cloned.1.call-done = bf16[32,2816]{1,0:T(8,128)(2,1)} async-done(((bf16[1024,2816]{1,0:T(8,128)(2,1)}), bf16[32,2816]{1,0:T(8,128)(2,1)}) %reduce-scatter.9.cloned.1.call-update) | async-done | bytes 180240 | tf_op jit(solution)/shard_map/reduce_scatter | solution.py:53
  1397.8 1.8 fusion.68
  1401.5 36.8 %psum.7 = f32[]{:T(128)} all-reduce(f32[]{:T(128)S(6)} %add.99), channel_id=1, replica_groups=mesh['rep'=1,'dp'=32] {'dp'}, use_global_device_ids=true, to_apply=%region_12.13 | all-reduce | flops 1 | bytes 8 | tf_op jit(solution)/shard_map/psum | solution.py:55
  1439.1 2.4 fusion.76
  1441.5 4.0 fusion.67
  (49 shorter events, 0.6 us)
Async XLA Ops:
  7.2 74.8 %all-gather.13.cloned.1.call-start = ((), (), s32[]{:S(2)}) async-start(), calls=%async_computation.12 | async-start | bytes 5947392 | tf_op jit(solution)/shard_map/all_gather | solution.py:40
  9.0 142.5 %all-gather.15.cloned.1.call-start = ((), (), s32[]{:S(2)}) async-start(), calls=%async_computation.13 | async-start | bytes 5947392 | tf_op jit(solution)/shard_map/all_gather | solution.py:40
  10.8 210.3 %all-gather.17.cloned.1.call-start = ((), (), s32[]{:S(2)}) async-start(), calls=%async_computation.14 | async-start | bytes 5947392 | tf_op jit(solution)/shard_map/all_gather | solution.py:40
  12.7 277.9 %all-gather.21.cloned.1.call-start = ((), (), s32[]{:S(2)}) async-start(), calls=%async_computation.16 | async-start | bytes 5947392 | tf_op jit(solution)/shard_map/all_gather | solution.py:40
  13.3 346.7 %all-gather.23.cloned.1.call-start = ((), (), s32[]{:S(2)}) async-start(), calls=%async_computation.17 | async-start | bytes 5947392 | tf_op jit(solution)/shard_map/all_gather | solution.py:40
  13.9 415.6 %all-gather.19.cloned.1.call-start = ((), (), s32[]{:S(2)}) async-start(), calls=%async_computation.15 | async-start | bytes 5947392 | tf_op jit(solution)/shard_map/all_gather | solution.py:40
  14.4 657.0 %reduce-scatter.15.cloned.1.call-start = ((), (), s32[]{:S(2)}) async-start(), calls=%async_computation.10 | async-start | bytes 5947392 | tf_op jit(solution)/shard_map/reduce_scatter | solution.py:53
  24.1 127.5 %copy-start.13 = (f32[2048]{0:T(1024)}, f32[2048]{0:T(1024)S(1)}, u32[]{:S(2)}) copy-start(f32[2048]{0:T(1024)S(1)} %add_rsqrt_fusion) | copy-start | bytes 24580
  240.9 67.8 %copy-start.11 = (f32[2048]{0:T(1024)}, f32[2048]{0:T(1024)S(1)}, u32[]{:S(2)}) copy-start(f32[2048]{0:T(1024)S(1)} %get-tuple-element.26) | copy-start | bytes 24580
  240.9 263.5 %copy-start.9 = (f32[2048]{0:T(1024)}, f32[2048]{0:T(1024)S(1)}, u32[]{:S(2)}) copy-start(f32[2048]{0:T(1024)S(1)} %fusion.80) | copy-start | bytes 24580
  485.5 18.9 %copy-start.12 = (f32[2048]{0:T(1024)S(1)}, f32[2048]{0:T(1024)}, u32[]{:S(2)}) copy-start(f32[2048]{0:T(1024)} %copy-done.11) | copy-start | bytes 24580
  485.5 18.9 %copy-start = (bf16[1,2048,1024]{1,2,0:T(8,128)(2,1)S(1)}, bf16[1,2048,1024]{1,2,0:T(8,128)(2,1)}, u32[]{:S(2)}) copy-start(bf16[1,2048,1024]{1,2,0:T(8,128)(2,1)} %copy.21) | copy-start | bytes 12582916
  485.5 18.9 %copy-start.1 = (bf16[2048,1024]{0,1:T(8,128)(2,1)S(1)}, bf16[2048,1024]{0,1:T(8,128)(2,1)}, u32[]{:S(2)}) copy-start(bf16[2048,1024]{0,1:T(8,128)(2,1)} %get-tuple-element.27) | copy-start | bytes 12582916
  508.0 2.0 copy-start.2
  527.2 289.4 %reduce-scatter.17.cloned.1.call-start = ((), (), s32[]{:S(2)}) async-start(), calls=%async_computation.11 | async-start | bytes 5947392 | tf_op jit(solution)/shard_map/reduce_scatter | solution.py:53
  550.8 18.6 %copy-start.14 = (f32[2048]{0:T(1024)S(1)}, f32[2048]{0:T(1024)}, u32[]{:S(2)}) copy-start(f32[2048]{0:T(1024)} %copy-done.13) | copy-start | bytes 24580
  550.8 411.2 %reduce-scatter.11.cloned.1.call-start = ((), (), s32[]{:S(2)}) async-start(), calls=%async_computation.8 | async-start | bytes 5947392 | tf_op jit(solution)/shard_map/reduce_scatter | solution.py:53
  569.4 22.6 %copy-start.10 = (f32[2048]{0:T(1024)S(1)}, f32[2048]{0:T(1024)}, u32[]{:S(2)}) copy-start(f32[2048]{0:T(1024)} %copy-done.9) | copy-start | bytes 24580
  591.9 515.3 %reduce-scatter.13.cloned.1.call-start = ((), (), s32[]{:S(2)}) async-start(), calls=%async_computation.9 | async-start | bytes 5947392 | tf_op jit(solution)/shard_map/reduce_scatter | solution.py:53
  614.7 637.8 %reduce-scatter.7.cloned.1.call-start = ((), (), s32[]{:S(2)}) async-start(), calls=%async_computation.6 | async-start | bytes 5947392 | tf_op jit(solution)/shard_map/reduce_scatter | solution.py:53
  641.8 797.2 %copy-start.5 = (bf16[2,88,1024]{2,1,0:T(8,128)(2,1)S(1)}, bf16[2,88,1024]{2,1,0:T(8,128)(2,1)}, u32[]{:S(2)}) copy-start(bf16[2,88,1024]{2,1,0:T(8,128)(2,1)} %param.15) | copy-start | bytes 1081348
  641.8 797.2 %copy-start.6 = (f32[2,88,1024]{2,1,0:T(8,128)S(1)}, f32[2,88,1024]{2,1,0:T(8,128)}, u32[]{:S(2)}) copy-start(f32[2,88,1024]{2,1,0:T(8,128)} %param.21) | copy-start | bytes 2162692
  641.8 797.2 %copy-start.7 = (f32[2,88,1024]{2,1,0:T(8,128)S(1)}, f32[2,88,1024]{2,1,0:T(8,128)}, u32[]{:S(2)}) copy-start(f32[2,88,1024]{2,1,0:T(8,128)} %param.18) | copy-start | bytes 2162692
  641.9 755.9 %reduce-scatter.9.cloned.1.call-start = ((), (), s32[]{:S(2)}) async-start(), calls=%async_computation.7 | async-start | bytes 5947392 | tf_op jit(solution)/shard_map/reduce_scatter | solution.py:53
  660.9 780.6 %copy-start.3 = (bf16[2,32,2816]{2,1,0:T(8,128)(2,1)S(1)}, bf16[2,32,2816]{2,1,0:T(8,128)(2,1)}, u32[]{:S(2)}) copy-start(bf16[2,32,2816]{2,1,0:T(8,128)(2,1)} %param.13) | copy-start | bytes 1081348
  660.9 780.6 %copy-start.4 = (bf16[2,32,2816]{2,1,0:T(8,128)(2,1)S(1)}, bf16[2,32,2816]{2,1,0:T(8,128)(2,1)}, u32[]{:S(2)}) copy-start(bf16[2,32,2816]{2,1,0:T(8,128)(2,1)} %param.14) | copy-start | bytes 1081348
  660.9 780.6 %copy-start.8 = (f32[2,32,2816]{2,1,0:T(8,128)S(1)}, f32[2,32,2816]{2,1,0:T(8,128)}, u32[]{:S(2)}) copy-start(f32[2,32,2816]{2,1,0:T(8,128)} %param.19) | copy-start | bytes 2162692
Sparse Core Ops, SparseCore 0:
  11.4 70.4 all-gather.12
  85.4 66.1 all-gather.14
  155.0 66.1 all-gather.16
  224.4 66.1 all-gather.20
  293.9 66.1 all-gather.22
  363.3 66.1 all-gather.18
  527.3 144.0 reduce-scatter.14
  673.8 142.8 reduce-scatter.16
  818.9 143.0 reduce-scatter.10
  964.2 142.9 reduce-scatter.12
  1109.5 142.9 reduce-scatter.6
  1254.7 142.9 reduce-scatter.8
where the time goes:
time: 1460 us; the launch traced here: 1450 us
  waiting for transfers between devices  1030 us (71%)
  matrix products  331 us (23%)
  blocking collectives  36.8 us (3%)
  local copies, waits for them, and re-layouts  20.4 us (1%)
  other arithmetic  18.5 us (1%)
  between operations  17.5 us (1%)
    reduce_scatter x6, waiting for transfers between devices, step(): lax.psum_scatter(by_w[name], 'dp', scatter_dimension=0, tiled=True)  733 us
    all_gather x6, waiting for transfers between devices, fetched(): lax.all_gather(w[number], 'dp', axis=0, tiled=True)  293 us
    dot_general x5, matrix products, layer(): gate = jnp.dot(a, w['w_gate'], preferred_element_type=jnp.float32)  119 us
    dot_general x5, matrix products, layer(): up = jnp.dot(a, w['w_up'], preferred_element_type=jnp.float32)  115 us
    dot_general x5, matrix products, matmul(): jnp.dot(a, w, preferred_element_type=jnp.float32).astype(jnp.bfloat16)  97.1 us
    psum x1, blocking collectives, step(): squares = lax.psum(sum((jnp.sum(g * g) for g in gradients)), 'dp')  36.8 us
  transfers between devices with their start and end apart: 12, of which 12 were waited for; matrix products, arithmetic and copies ran while one was open for 18% of the time, Pallas kernels for 0%

commit v1 on v0

v1 whole, which is shorter than its diff:
```python
import functools

import jax
import jax.numpy as jnp
from jax import lax
from jax.experimental import pallas as pl
from jax.experimental.pallas import tpu as pltpu
from jax.sharding import PartitionSpec as P

NAMES = ("w_gate", "w_up", "w_down")
F32, BF16 = jnp.float32, jnp.bfloat16
MESH = pl.DeviceIdType.MESH


def matmul(a, w):
    return jnp.dot(a, w, preferred_element_type=F32).astype(BF16)


def normed(h):
    wide = h.astype(F32)
    scale = lax.rsqrt(jnp.mean(wide**2, -1, keepdims=True) + 1e-6)
    return (wide * scale).astype(BF16)


def layer(h, w):
    a = normed(h)
    gate = jnp.dot(a, w["w_gate"], preferred_element_type=F32)
    up = jnp.dot(a, w["w_up"], preferred_element_type=F32)
    return h + matmul((jax.nn.silu(gate) * up).astype(BF16), w["w_down"])


def adamw(w, m, v, g):
    m = 0.9 * m + 0.1 * g
    v = 0.95 * v + 0.05 * g * g
    step = m * lax.rsqrt(v + 1e-8) + 0.1 * w
    return (w - 0.02 * step).astype(BF16), m, v


class Place:
    def __init__(self):
        d = lax.axis_index("dp")
        self.c, self.z, self.y, self.x = d % 2, (d // 2) % 4, (d // 8) % 2, d // 16
        self.own, self.xs, self.ys = self.x * 2 + self.y, (1 - self.x) * 2 + self.y, self.x * 2 + 1 - self.y
        self.diag = (1 - self.x) * 2 + 1 - self.y

    def at(self, plane, z, c):
        return {"dp": (plane * 4 + z) * 2 + c}

    def to_x(self):
        return self.at(self.xs, self.z, self.c)

    def to_y(self):
        return self.at(self.ys, self.z, self.c)

    def to_c(self):
        return self.at(self.own, self.z, 1 - self.c)

    def to_z(self, k):
        return self.at(self.own, (self.z + k) % 4, self.c)

    def partners(self):
        return [self.to_x(), self.to_y(), self.to_c()] + [self.to_z(k) for k in (1, 2, 3)]


def greet(place):
    barrier = pltpu.get_barrier_semaphore()
    for device in place.partners():
        pl.semaphore_signal(barrier, inc=1, device_id=device, device_id_type=MESH)
    pl.semaphore_wait(barrier, 6)


def send(src, dst, send_sem, recv_sem, device):
    pltpu.make_async_remote_copy(src, dst, send_sem, recv_sem, device_id=device, device_id_type=MESH).start()


def await_bytes(ref, sem):
    pltpu.make_async_copy(ref, ref, sem).wait()


class Gather:
    Z, XA, XB, YA, YB, DX, DY, C, OWN, SENT = range(10)
    SEMS = 10

    def __init__(self, place, mine, out, sems):
        self.p, self.mine, self.out, self.sems = place, mine, out, sems

    def along_z(self):
        p = self.p
        here = self.out.at[p.own, p.z, p.c]
        for k in (1, 2, 3):
            send(self.mine, here, self.sems.at[self.SENT], self.sems.at[self.Z], p.to_z(k))
        pltpu.make_async_copy(self.mine, here, self.sems.at[self.OWN]).start()

    def _move(self, plane, zs, slot, device):
        ref = self.out.at[plane, zs, self.p.c]
        send(ref, ref, self.sems.at[self.SENT], self.sems.at[slot], device)

    def _arrived(self, plane, zs, slot):
        await_bytes(self.out.at[plane, zs, self.p.c], self.sems.at[slot])

    def to_plane(self):
        p, lo, hi, al = self.p, pl.ds(0, 2), pl.ds(2, 2), pl.ds(0, 4)
        await_bytes(self.out.at[p.own, pl.ds(0, 3), p.c], self.sems.at[self.Z])
        await_bytes(self.out.at[p.own, p.z, p.c], self.sems.at[self.OWN])
        self._move(p.own, lo, self.XA, p.to_x())
        self._move(p.own, hi, self.YB, p.to_y())
        self._move(p.own, hi, self.XB, p.to_x())
        self._move(p.own, lo, self.YA, p.to_y())
        self._move(p.own, al, self.C, p.to_c())

    def across(self):
        p, lo, hi, al = self.p, pl.ds(0, 2), pl.ds(2, 2), pl.ds(0, 4)
        self._arrived(p.xs, lo, self.XA)
        self._move(p.xs, lo, self.DY, p.to_y())
        self._arrived(p.ys, hi, self.YB)
        self._move(p.ys, hi, self.DX, p.to_x())
        self._arrived(p.xs, hi, self.XB)
        self._move(p.xs, al, self.C, p.to_c())
        self._arrived(p.ys, lo, self.YA)
        self._move(p.ys, al, self.C, p.to_c())

    def to_core(self):
        p = self.p
        self._arrived(p.diag, pl.ds(0, 2), self.DY)
        self._arrived(p.diag, pl.ds(2, 2), self.DX)
        self._move(p.diag, pl.ds(0, 4), self.C, p.to_c())

    def done(self):
        await_bytes(self.out.at[:, :, 0], self.sems.at[self.C])

    def sent(self):
        p = self.p
        for _ in range(3):
            await_bytes(self.mine, self.sems.at[self.SENT])
        for _ in range(7):
            await_bytes(self.out.at[0, :, 0], self.sems.at[self.SENT])


def gather_all(blocks):
    n = len(blocks)
    halves = [(i, half) for i in range(n) for half in range(2)]

    def kernel(*refs):
        ins, outs, held, (load_sem, sems) = refs[:n], refs[n : 2 * n], refs[2 * n : 3 * n], refs[3 * n :]
        place = Place()
        for i in range(n):
            pltpu.make_async_copy(ins[i], held[i], load_sem.at[i]).start()
        greet(place)
        jobs = []
        for j, (i, half) in enumerate(halves):
            w = blocks[i].shape[1] // 2
            cols = pl.ds(half * w, w)
            jobs.append(Gather(place, held[i].at[:, cols], outs[i].at[:, :, :, :, cols], sems.at[j]))
        for j, (i, half) in enumerate(halves):
            if half == 0:
                pltpu.make_async_copy(ins[i], held[i], load_sem.at[i]).wait()
            jobs[j].along_z()
        for s in range(len(jobs) + 2):
            if s < len(jobs):
                jobs[s].to_plane()
            if 0 <= s - 1 < len(jobs):
                jobs[s - 1].across()
            if 0 <= s - 2 < len(jobs):
                jobs[s - 2].to_core()
        for job in jobs:
            job.done()
            job.sent()

    outs = pl.pallas_call(
        kernel,
        name="gather_all",
        in_specs=[pl.BlockSpec(memory_space=pl.ANY)] * n,
        out_specs=[pl.BlockSpec(memory_space=pl.ANY)] * n,
        out_shape=[jax.ShapeDtypeStruct((4, 4, 2) + b.shape, BF16) for b in blocks],
        scratch_shapes=[pltpu.VMEM(b.shape, BF16) for b in blocks]
        + [pltpu.SemaphoreType.DMA((n,)), pltpu.SemaphoreType.DMA((len(halves), Gather.SEMS))],
        compiler_params=pltpu.CompilerParams(collective_id=0, has_side_effects=True),
    )(*blocks)
    return [o.reshape(32 * b.shape[0], b.shape[1]) for o, b in zip(outs, blocks, strict=True)]


def add_into(dst, *srcs):
    n, r, w = dst.shape

    def rows(i, _):
        total = srcs[0][i].astype(F32)
        for s in srcs[1:]:
            total += s[i].astype(F32)
        dst[i] = total.astype(dst.dtype)
        return 0

    for i in range(n):
        rows(i, 0)


class Scatter:
    C, L, P1X, P1Y, XA, XB, YA, YB, Z, SENT = 0, 4, 8, 9, 10, 11, 12, 13, 14, 15
    SEMS = 16

    @staticmethod
    def scratch(r, w):
        return [pltpu.VMEM((4, 4, r, w), BF16), pltpu.VMEM((4, 4, r, w), BF16), pltpu.VMEM((15, r, w), BF16)]

    def __init__(self, place, terms, out, mine, other, arrived, sems):
        self.p, self.terms, self.out, self.mine, self.other, self.sems = place, terms, out, mine, other, sems
        self.p1x, self.p1y = arrived.at[pl.ds(0, 2)], arrived.at[pl.ds(2, 2)]
        self.rx, self.ry, self.rz = arrived.at[pl.ds(4, 4)], arrived.at[pl.ds(8, 4)], arrived.at[pl.ds(12, 3)]

    def start(self):
        p = self.p
        for g, plane in enumerate((p.diag, p.xs, p.ys, p.own)):
            send(self.terms.at[plane, :, 1 - p.c], self.other.at[g], self.sems.at[self.SENT], self.sems.at[self.C + g], p.to_c())
            pltpu.make_async_copy(self.terms.at[plane, :, p.c], self.mine.at[g], self.sems.at[self.L + g]).start()

    def _both(self, g):
        await_bytes(self.other.at[g], self.sems.at[self.C + g])
        await_bytes(self.mine.at[g], self.sems.at[self.L + g])

    def _send(self, src, dst, slot, device):
        send(src, dst, self.sems.at[self.SENT], self.sems.at[slot], device)

    def diagonal(self):
        p, lo, hi = self.p, pl.ds(0, 2), pl.ds(2, 2)
        self._both(0)
        add_into(self.mine.at[0], self.mine.at[0], self.other.at[0])
        self._send(self.mine.at[0, lo], self.p1x, self.P1X, p.to_x())
        self._send(self.mine.at[0, hi], self.p1y, self.P1Y, p.to_y())

    def straight(self):
        p, lo, hi = self.p, pl.ds(0, 2), pl.ds(2, 2)
        self._both(1)
        add_into(self.mine.at[1, lo], self.mine.at[1, lo], self.other.at[1, lo])
        self._send(self.mine.at[1, lo], self.rx.at[lo], self.XA, p.to_x())
        self._both(2)
        add_into(self.mine.at[2, hi], self.mine.at[2, hi], self.other.at[2, hi])
        self._send(self.mine.at[2, hi], self.ry.at[hi], self.YB, p.to_y())

    def joined(self):
        p, lo, hi = self.p, pl.ds(0, 2), pl.ds(2, 2)
        await_bytes(self.p1y, self.sems.at[self.P1Y])
        add_into(self.mine.at[1, hi], self.mine.at[1, hi], self.other.at[1, hi], self.p1y)
        self._send(self.mine.at[1, hi], self.rx.at[hi], self.XB, p.to_x())
        await_bytes(self.p1x, self.sems.at[self.P1X])
        add_into(self.mine.at[2, lo], self.mine.at[2, lo], self.other.at[2, lo], self.p1x)
        self._send(self.mine.at[2, lo], self.ry.at[lo], self.YA, p.to_y())

    def along_z(self):
        p, lo, hi = self.p, pl.ds(0, 2), pl.ds(2, 2)
        self._both(3)
        for part, xs, ys in ((lo, self.XA, self.YA), (hi, self.XB, self.YB)):
            await_bytes(self.rx.at[part], self.sems.at[xs])
            await_bytes(self.ry.at[part], self.sems.at[ys])
            add_into(self.mine.at[3, part], self.mine.at[3, part], self.other.at[3, part], self.rx.at[part], self.ry.at[part])
        for k in (1, 2, 3):
            self._send(self.mine.at[3, (p.z + k) % 4], self.rz.at[k - 1], self.Z, p.to_z(k))

    def last(self):
        await_bytes(self.rz, self.sems.at[self.Z])
        total = self.mine[3, self.p.z].astype(F32)
        for k in range(3):
            total += self.rz[k].astype(F32)
        g = total.astype(BF16)
        self.out[...] = g
        g = g.astype(F32)
        return jnp.sum(g * g)

    def sent(self):
        for _ in range(4):
            await_bytes(self.other.at[0], self.sems.at[self.SENT])
        for _ in range(3):
            await_bytes(self.other.at[0], self.sems.at[self.SENT])
        await_bytes(self.rz, self.sems.at[self.SENT])


def scatter_all(terms):
    n = len(terms)
    shapes = [(t.shape[0] // 32, t.shape[1]) for t in terms]
    halves = [(i, half) for i in range(n) for half in range(2)]
    nj = len(halves)

    def kernel(*refs):
        ins, outs, squares, rest = refs[:n], refs[n : 2 * n], refs[2 * n], refs[2 * n + 1 :]
        bufs, (sums, gone, sums_sem, sems) = rest[: 3 * nj], rest[3 * nj :]
        place = Place()
        greet(place)
        jobs = []
        for j, (i, half) in enumerate(halves):
            w = shapes[i][1] // 2
            cols = pl.ds(half * w, w)
            jobs.append(Scatter(place, ins[i].at[:, :, :, :, cols], outs[i].at[:, cols], *bufs[3 * j : 3 * j + 3], sems.at[j]))
        total = jnp.float32(0)
        for t in range(-2, nj + 2):
            for offset, stage in ((2, Scatter.start), (1, Scatter.diagonal), (1, Scatter.straight), (0, Scatter.joined), (-1, Scatter.along_z)):
                if 0 <= t + offset < nj:
                    stage(jobs[t + offset])
            if 0 <= t - 2 < nj:
                total += jobs[t - 2].last()
        sums[0] = jnp.full((8, 128), total, F32)
        for i, device in enumerate((place.to_c(), place.to_x(), place.to_y())):
            send(sums.at[i], gone.at[i], sums_sem.at[0], sums_sem.at[1 + i], device)
            await_bytes(gone.at[i], sums_sem.at[1 + i])
            sums[i + 1] = sums[i] + gone[i]
        for k in (1, 2, 3):
            send(sums.at[3], gone.at[2 + k], sums_sem.at[0], sums_sem.at[4], place.to_z(k))
        await_bytes(gone.at[pl.ds(3, 3)], sums_sem.at[4])
        squares[...] = (sums[3] + gone[3]) + (gone[4] + gone[5])
        await_bytes(gone, sums_sem.at[0])
        for job in jobs:
            job.sent()

    scratch = []
    for i, _ in halves:
        scratch += Scatter.scratch(shapes[i][0], shapes[i][1] // 2)
    scratch += [pltpu.VMEM((4, 8, 128), F32), pltpu.VMEM((6, 8, 128), F32), pltpu.SemaphoreType.DMA((5,)), pltpu.SemaphoreType.DMA((nj, Scatter.SEMS))]
    *outs, squares = pl.pallas_call(
        kernel,
        name="scatter_all",
        in_specs=[pl.BlockSpec(memory_space=pl.ANY)] * n,
        out_specs=[pl.BlockSpec(memory_space=pltpu.VMEM)] * (n + 1),
        out_shape=[jax.ShapeDtypeStruct(s, BF16) for s in shapes] + [jax.ShapeDtypeStruct((8, 128), F32)],
        scratch_shapes=scratch,
        compiler_params=pltpu.CompilerParams(collective_id=1, has_side_effects=True, vmem_limit_bytes=66_000_000),
    )(*[t.reshape((4, 4, 2) + s) for t, s in zip(terms, shapes, strict=True)])
    return outs, squares


def solution(mesh):
    def step(x, dy, *arrays):
        weights, m, v = (arrays[i : i + 3] for i in (0, 3, 6))
        layers = weights[0].shape[0]
        flat = gather_all([w[number] for number in range(layers) for w in weights])
        full = [dict(zip(NAMES, flat[3 * number : 3 * number + 3], strict=True)) for number in range(layers)]
        h, kept = x[0], []
        for number in range(layers):
            kept.append(h)
            h = layer(h, full[number])
        by_h, terms = dy[0], []
        for number in reversed(range(layers)):
            _, back = jax.vjp(layer, kept[number], full[number])
            by_h, by_w = back(by_h)
            terms += [by_w[name] for name in ("w_down", "w_gate", "w_up")]
        sums, squares = scatter_all(terms)
        sums = {(number, name): sums[3 * (layers - 1 - number) + k] for number in range(layers) for k, name in enumerate(("w_down", "w_gate", "w_up"))}
        gradients = [jnp.stack([sums[number, name] for number in range(layers)]).astype(F32) for name in NAMES]
        count = 32 * sum(g.size for g in gradients)
        factor = jnp.minimum(1.0, 0.5 * lax.rsqrt(squares[0, 0] / count + 1e-30))
        new = [adamw(w.astype(F32), m, v, g * factor) for w, m, v, g in zip(weights, m, v, gradients, strict=True)]
        return tuple(one[which] for which in range(3) for one in new)

    states, cut = P(("rep", "dp"), None, None), P(None, "dp", None)
    return jax.shard_map(
        step,
        mesh=mesh,
        in_specs=(states, states) + (cut,) * 9,
        out_specs=(P("rep", "dp", None),) * 9,
        check_vma=False,
    )
```

time: 1460 us -> 700 us (0.48)
  waiting for transfers between devices: 1030 us -> 0 us
  Pallas kernels: 0 us -> 333 us
  blocking collectives: 36.8 us -> 0 us
  between operations: 17.5 us -> 1.93 us
    reduce_scatter x6 -> x0, waiting for transfers between devices: 733 us -> none  [step(): lax.psum_scatter(by_w[name], 'dp', scatter_dimension=0, tiled=True)]
    pallas_call x0 -> x2, Pallas kernels: none -> 333 us  [the longest x1 175 us: scatter_all(): pl.pallas_call(kernel, name='scatter_all', in_specs=[pl.BlockSpec(memory_...]
    all_gather x6 -> x0, waiting for transfers between devices: 293 us -> none  [fetched(): lax.all_gather(w[number], 'dp', axis=0, tiled=True)]
    psum x1 -> x0, blocking collectives: 36.8 us -> none  [step(): squares = lax.psum(sum((jnp.sum(g * g) for g in gradients)), 'dp')]
  transfers between devices with their start and end apart: 12 -> 0, of which waited for: 12 -> 0; matrix products, arithmetic and copies ran while one was open for 18% -> 0% of each run, Pallas kernels for 0% -> 0%
where the time goes in v1:
time: 700 us; the launch traced here: 693 us
  Pallas kernels  333 us (48%)
  matrix products  322 us (46%)
  local copies, waits for them, and re-layouts  18.2 us (3%)
  other arithmetic  17.7 us (3%)
    pallas_call x1, Pallas kernels, scatter_all(): pl.pallas_call(kernel, name='scatter_all', in_specs=[pl.BlockSpec(memory_...  175 us
    pallas_call x1, Pallas kernels, gather_all(): pl.pallas_call(kernel, name='gather_all', in_specs=[pl.BlockSpec(memory_s...  158 us
    dot_general x5, matrix products, layer(): up = jnp.dot(a, w['w_up'], preferred_element_type=F32)  114 us
    dot_general x5, matrix products, layer(): gate = jnp.dot(a, w['w_gate'], preferred_element_type=F32)  113 us
    dot_general x5, matrix products, matmul(): return jnp.dot(a, w, preferred_element_type=F32).astype(BF16)  94.8 us

profile of v1, /device:TPU:0, one launch (start us, length us, event | category | flops | bytes accessed | tf_op | source)
XLA Modules:
  0.0 692.7 jit_solution(6256858937430315170)
XLA Ops:
  0.6 2.1 slice_bitcast_fusion.1
  2.7 1.8 slice_bitcast_fusion
  4.5 157.8 %gather_all.1 = (bf16[4,4,2,32,2816]{4,3,2,1,0:T(8,128)(2,1)}, bf16[4,4,2,32,2816]{4,3,2,1,0:T(8,128)(2,1)}, bf16[4,4,2,88,1024]{4,3,2,1,0:T(8,128)(2,1)}, bf16[...) custom-call(bf16[32,2816]{1,0:T(8,128)(2,1)} %get-tuple-element.58.refs_0, ...), custom_call_target="tpu_custom_call" | custom-call | tf_op jit(solution)/shard_map/gather_all/pallas_call | solution.py:169
  162.3 6.5 copy.20
  168.8 3.1 fusion.15
  171.9 0.0 copy-start.10
  171.9 0.0 copy-start.2
  171.9 20.0 %fusion.43 = f32[2048,2816]{1,0:T(8,128)} fusion(bf16[1024,2816]{1,0:T(8,128)(2,1)} %bitcast.97, bf16[1,2048,1024]{2,1,0:T(8,128)(2,1)} %param.11, f32[2048]{0:T(1024)S(1)} %add_rsqrt_fusion), kind=kOutput, calls=%fused_computation.56 | convolution fusion | flops 11817451520 | bytes 33038336 | tf_op jit(solution)/shard_map/dot_general | solution.py:27
  191.9 0.0 copy-done.10
  191.9 0.0 copy-done.2
  191.9 26.6 %multiply_convert_fusion.1 = (bf16[2048,2816]{1,0:T(8,128)(2,1)}, f32[2048,2816]{1,0:T(8,128)}) fusion(f32[2048,2816]{1,0:T(8,128)} %fusion.43, bf16[1024,2816]{1,0:T(8,128)(2,1)} %bitcast.96, bf16[1,2048,1024]{2,1,0:T(8,128)(2,1)S(1)} %copy-done.2, f32[2048]{0:T(1024)S(1)} %add_rsqrt_fusion), kind=kOutput, calls=%fused_computation.17 | convolution fusion | flops 11852054528 | bytes 67641344 | tf_op jit(solution)/shard_map/dot_general | solution.py:28
  218.5 19.7 %fusion.19 = (f32[2048]{0:T(1024)S(1)}, bf16[2048,1024]{0,1:T(8,128)(2,1)}) fusion(bf16[2048,2816]{1,0:T(8,128)(2,1)} %get-tuple-element.50, bf16[2816,1024]{1,0:T(8,128)(2,1)} %bitcast.87, bf16[1,2048,1024]{1,2,0:T(8,128)(2,1)} %copy.20), kind=kOutput, calls=%fused_computation.37 | convolution fusion | flops 11821643776 | bytes 25698304 | tf_op jit(solution)/shard_map/dot_general | solution.py:16
  238.2 0.0 copy-start.3
  238.2 0.0 slice-start
  238.2 20.7 %fusion.37 = f32[2048,2816]{1,0:T(8,128)} fusion(bf16[1024,2816]{1,0:T(8,128)(2,1)} %bitcast.93, bf16[2048,1024]{0,1:T(8,128)(2,1)} %get-tuple-element.53, f32[2048]{0:T(1024)S(1)} %fusion.57), kind=kOutput, calls=%fused_computation.53 | convolution fusion | flops 11817451520 | bytes 33038336 | tf_op jit(solution)/shard_map/jvp()/dot_general | solution.py:28
  258.9 0.0 copy-done.8
  258.9 0.0 copy-done.3
  258.9 0.0 slice-start.1
  258.9 17.2 %convolution_convert_fusion.1 = bf16[2816,2048]{0,1:T(8,128)(2,1)} fusion(bf16[2816,1024]{1,0:T(8,128)(2,1)} %bitcast.95, bf16[1,2048,1024]{2,1,0:T(8,128)(2,1)S(1)} %copy-done.3), kind=kOutput, calls=%fused_computation.29 | convolution fusion | flops 11816927232 | bytes 21495808 | tf_op jit(solution)/shard_map/transpose(jvp())/dot_general | solution.py:16
  276.1 0.0 slice-done
  276.1 0.0 copy-done.1
  276.1 0.0 slice-done.1
  276.1 30.0 %fusion.2 = (bf16[2048,2816]{1,0:T(8,128)(2,1)}, f32[2048,2816]{1,0:T(8,128)}) fusion(f32[2048,2816]{1,0:T(8,128)} %fusion.37, bf16[2816,2048]{0,1:T(8,128)(2,1)} %convolution_convert_fusion.1, bf16[1024,2816]{1,0:T(8,128)(2,1)S(1)} %bitcast.92, bf16[2048,1024]{0,1:T(8,128)(2,1)S(1)} %copy-done.1, f32[2048]{0:T(1024)S(1)} %fusion.57), kind=kOutput, calls=%fused_computation.6 | convolution fusion | flops 11886657536 | bytes 79175680 | tf_op jit(solution)/shard_map/jvp()/dot_general | solution.py:27
  306.1 23.6 %fusion.22 = bf16[2816,1024]{1,0:T(8,128)(2,1)} fusion(f32[2048,2816]{1,0:T(8,128)} %fusion.37, bf16[1,2048,1024]{2,1,0:T(8,128)(2,1)} %param.12, f32[2048,2816]{1,0:T(8,128)} %get-tuple-element.55), kind=kOutput, calls=%fused_computation.41 | convolution fusion | flops 11848646656 | bytes 56098816 | tf_op jit(solution)/shard_map/transpose(jvp())/dot_general | solution.py:16
  329.7 17.8 %convolution_convert_fusion.3 = bf16[1024,2816]{1,0:T(8,128)(2,1)} fusion(bf16[2048,2816]{1,0:T(8,128)(2,1)} %get-tuple-element.54, bf16[2048,1024]{0,1:T(8,128)(2,1)S(1)} %copy-done.1, f32[2048]{0:T(1024)S(1)} %fusion.57), kind=kOutput, calls=%fused_computation.46 | convolution fusion | flops 11817451520 | bytes 21504000 | tf_op jit(solution)/shard_map/transpose(jvp())/dot_general | solution.py:27
  347.5 22.4 %fusion.23 = bf16[1024,2816]{1,0:T(8,128)(2,1)} fusion(bf16[2816,2048]{0,1:T(8,128)(2,1)} %convolution_convert_fusion.1, bf16[2048,1024]{0,1:T(8,128)(2,1)} %get-tuple-element.53, f32[2048]{0:T(1024)S(1)} %fusion.57, f32[2048,2816]{1,0:T(8,128)} %get-tuple-element.55), kind=kOutput, calls=%fused_computation.42 | convolution fusion | flops 11854938112 | bytes 44572672 | tf_op jit(solution)/shard_map/transpose(jvp())/dot_general | solution.py:28
  369.9 21.8 %fusion.11 = bf16[2048,1024]{0,1:T(8,128)(2,1)} fusion(bf16[1024,2816]{1,0:T(8,128)(2,1)} %bitcast.94, bf16[2816,2048]{0,1:T(8,128)(2,1)} %convolution_convert_fusion.1, f32[2048,2816]{1,0:T(8,128)} %get-tuple-element.55), kind=kOutput, calls=%fused_computation.20 | convolution fusion | flops 11845763072 | bytes 44564480 | tf_op jit(solution)/shard_map/transpose(jvp())/dot_general | solution.py:28
  391.7 20.3 %fusion.21 = (f32[2048]{0:T(1024)S(1)}, bf16[2048,1024]{0,1:T(8,128)(2,1)}) fusion(bf16[2048,1024]{0,1:T(8,128)(2,1)} %get-tuple-element.53, bf16[2048,1024]{0,1:T(8,128)(2,1)} %fusion.11, bf16[2048,2816]{1,0:T(8,128)(2,1)} %get-tuple-element.54, bf16[1024,2816]{1,0:T(8,128)(2,1)} %bitcast.89), kind=kOutput, calls=%fused_computation.39 | convolution fusion | flops 11821643776 | bytes 29892608 | tf_op jit(solution)/shard_map/transpose(jvp())/dot_general | solution.py:27
  412.0 6.5 copy.21
  418.5 0.0 copy-done.9
  418.5 6.2 fusion.29
  424.7 17.0 %convolution_convert_fusion.2 = bf16[2816,1024]{1,0:T(8,128)(2,1)} fusion(bf16[2048,2816]{1,0:T(8,128)(2,1)} %get-tuple-element.50, bf16[2048,1024]{0,1:T(8,128)(2,1)S(1)} %fusion.29), kind=kOutput, calls=%fused_computation.45 | convolution fusion | flops 11814043648 | bytes 21495808 | tf_op jit(solution)/shard_map/transpose(jvp())/dot_general | solution.py:16
  441.8 17.3 %convolution_convert_fusion = bf16[2048,2816]{1,0:T(8,128)(2,1)} fusion(bf16[2048,1024]{0,1:T(8,128)(2,1)S(1)} %fusion.29, bf16[2816,1024]{1,0:T(8,128)(2,1)} %bitcast.88), kind=kOutput, calls=%fused_computation.28 | convolution fusion | flops 11816927232 | bytes 21495808 | tf_op jit(solution)/shard_map/transpose(jvp())/dot_general | solution.py:16
  459.1 0.0 copy-done
  459.1 0.0 copy-done.11
  459.1 24.9 %fusion.24 = bf16[1024,2816]{1,0:T(8,128)(2,1)} fusion(f32[2048,2816]{1,0:T(8,128)} %fusion.43, f32[2048,2816]{1,0:T(8,128)} %get-tuple-element.51, bf16[2048,2816]{1,0:T(8,128)(2,1)} %convolution_convert_fusion, bf16[1,2048,1024]{1,2,0:T(8,128)(2,1)S(1)} %copy-done, f32[2048]{0:T(1024)S(1)} %copy-done.11), kind=kOutput, calls=%fused_computation.43 | convolution fusion | flops 11883773952 | bytes 67641344 | tf_op jit(solution)/shard_map/transpose(jvp())/dot_general | solution.py:27
  484.1 22.7 %fusion.27 = bf16[1024,2816]{1,0:T(8,128)(2,1)} fusion(bf16[2048,2816]{1,0:T(8,128)(2,1)} %convolution_convert_fusion, f32[2048,2816]{1,0:T(8,128)} %fusion.43, bf16[1,2048,1024]{1,2,0:T(8,128)(2,1)} %copy.20, f32[2048]{0:T(1024)S(1)} %copy-done.11), kind=kOutput, calls=%fused_computation.44 | convolution fusion | flops 11854938112 | bytes 44572672 | tf_op jit(solution)/shard_map/transpose(jvp())/dot_general | solution.py:28
  506.7 0.0 copy-start.5
  506.7 0.0 copy-start.4
  506.8 175.1 %scatter_all.1 = (bf16[88,1024]{1,0:T(8,128)(2,1)}, bf16[32,2816]{1,0:T(8,128)(2,1)}, bf16[32,2816]{1,0:T(8,128)(2,1)}, bf16[88,1024]{1,0:T(8,128)(2,1)}, bf16[3...) custom-call(bf16[4,4,2,88,1024]{4,3,2,1,0:T(8,128)(2,1)} %bitcast.75, ...), custom_call_target="tpu_custom_call" | custom-call | tf_op jit(solution)/shard_map/scatter_all/pallas_call | solution.py:315
  681.9 0.0 copy-start.6
  681.9 0.0 copy-start.7
  681.9 1.3 slice.27
  683.9 0.0 copy-done.5
  683.9 2.9 fusion.47
  686.8 3.0 fusion.50
  689.8 0.0 copy-done.4
  689.8 2.5 fusion.53
  (11 shorter events, 0.0 us)
Async XLA Ops:
  171.9 20.1 %copy-start.10 = (f32[2048]{0:T(1024)}, f32[2048]{0:T(1024)S(1)}, u32[]{:S(2)}) copy-start(f32[2048]{0:T(1024)S(1)} %add_rsqrt_fusion) | copy-start | bytes 24580
  171.9 20.0 %copy-start.2 = (bf16[1,2048,1024]{2,1,0:T(8,128)(2,1)S(1)}, bf16[1,2048,1024]{2,1,0:T(8,128)(2,1)}, u32[]{:S(2)}) copy-start(bf16[1,2048,1024]{2,1,0:T(8,128)(2,1)} %param.11) | copy-start | bytes 12582916
  238.2 20.7 %copy-start.8 = (f32[2048]{0:T(1024)}, f32[2048]{0:T(1024)S(1)}, u32[]{:S(2)}) copy-start(f32[2048]{0:T(1024)S(1)} %get-tuple-element.52) | copy-start | bytes 24580
  238.2 20.7 %copy-start.3 = (bf16[1,2048,1024]{2,1,0:T(8,128)(2,1)S(1)}, bf16[1,2048,1024]{2,1,0:T(8,128)(2,1)}, u32[]{:S(2)}) copy-start(bf16[1,2048,1024]{2,1,0:T(8,128)(2,1)} %param.12) | copy-start | bytes 12582916
  238.2 37.9 %slice-start = ((s8[5767168]{0:T(1024)(128)(4,1)}), s8[4194304]{0:T(1024)(128)(4,1)S(1)}, s32[]{:S(2)}) async-start(s8[5767168]{0:T(1024)(128)(4,1)} %bitcast.90), calls=%async_computation | async-start | bytes 8388608
  258.9 17.2 %copy-start.1 = (bf16[2048,1024]{0,1:T(8,128)(2,1)S(1)}, bf16[2048,1024]{0,1:T(8,128)(2,1)}, u32[]{:S(2)}) copy-start(bf16[2048,1024]{0,1:T(8,128)(2,1)} %get-tuple-element.53) | copy-start | bytes 12582916
  258.9 17.2 %slice-start.1 = ((s8[5767168]{0:T(1024)(128)(4,1)}), s8[1572864]{0:T(1024)(128)(4,1)S(1)}, s32[]{:S(2)}) async-start(s8[5767168]{0:T(1024)(128)(4,1)} %bitcast.90), calls=%async_computation.1 | async-start | bytes 3145728
  412.0 6.5 copy-start.9
  441.8 17.4 %copy-start = (bf16[1,2048,1024]{1,2,0:T(8,128)(2,1)S(1)}, bf16[1,2048,1024]{1,2,0:T(8,128)(2,1)}, u32[]{:S(2)}) copy-start(bf16[1,2048,1024]{1,2,0:T(8,128)(2,1)} %copy.20) | copy-start | bytes 12582916
  441.8 17.4 %copy-start.11 = (f32[2048]{0:T(1024)S(1)}, f32[2048]{0:T(1024)}, u32[]{:S(2)}) copy-start(f32[2048]{0:T(1024)} %copy-done.10) | copy-start | bytes 24580
  506.7 177.2 %copy-start.5 = (bf16[2,32,2816]{2,1,0:T(8,128)(2,1)S(1)}, bf16[2,32,2816]{2,1,0:T(8,128)(2,1)}, u32[]{:S(2)}) copy-start(bf16[2,32,2816]{2,1,0:T(8,128)(2,1)} %param.13) | copy-start | bytes 1081348
  506.7 183.0 %copy-start.4 = (bf16[2,88,1024]{2,1,0:T(8,128)(2,1)S(1)}, bf16[2,88,1024]{2,1,0:T(8,128)(2,1)}, u32[]{:S(2)}) copy-start(bf16[2,88,1024]{2,1,0:T(8,128)(2,1)} %param.15) | copy-start | bytes 1081348
  681.9 7.9 %copy-start.6 = (f32[2,88,1024]{2,1,0:T(8,128)S(1)}, f32[2,88,1024]{2,1,0:T(8,128)}, u32[]{:S(2)}) copy-start(f32[2,88,1024]{2,1,0:T(8,128)} %param.21) | copy-start | bytes 2162692
  681.9 7.9 %copy-start.7 = (f32[2,88,1024]{2,1,0:T(8,128)S(1)}, f32[2,88,1024]{2,1,0:T(8,128)}, u32[]{:S(2)}) copy-start(f32[2,88,1024]{2,1,0:T(8,128)} %param.18) | copy-start | bytes 2162692

commit v2 on v0

v2 whole, which is shorter than its diff:
```python
import functools

import jax
import jax.numpy as jnp
from jax import lax
from jax.experimental import pallas as pl
from jax.experimental.pallas import tpu as pltpu
from jax.sharding import PartitionSpec as P

F32, BF16 = jnp.float32, jnp.bfloat16
MESH = pl.DeviceIdType.MESH
DEVICES, PLANE, LINE, TILE, LANES = 32, 4, 4, 256, 128
PAIR = 2
LO, HI, ALL = pl.ds(0, PAIR), pl.ds(PAIR, PAIR), pl.ds(0, LINE)
GRID = (PLANE, LINE, PAIR)
LEAD, TOOK, WIRE = 14, 24.0, 25.0
SHARES = ((2, 4, 5), (3, 3, 3, 2)), (2, 3, 3, 3)


def nn(a, b):
    return jnp.dot(a, b, preferred_element_type=F32)


def tn(a, b):
    return lax.dot_general(a, b, (((0,), (0,)), ((), ())), preferred_element_type=F32)


def nt(a, b):
    return lax.dot_general(a, b, (((1,), (1,)), ((), ())), preferred_element_type=F32)


def norm_scale(wide):
    return lax.rsqrt(jnp.mean(wide * wide, -1, keepdims=True) + 1e-6)


def norm_rows(h):
    wide = h.astype(F32)
    return (wide * norm_scale(wide)).astype(BF16)


def norm_back(da, h):
    wide, da = h.astype(F32), da.astype(F32)
    scale = norm_scale(wide)
    return (da * scale - wide * (scale * scale * scale * jnp.mean(da * wide, -1, keepdims=True))).astype(BF16)


def silu_back(gate, up, by_act):
    s = jax.nn.sigmoid(gate)
    return (by_act * up * s * (1 + gate * (1 - s))).astype(BF16), (by_act * gate * s).astype(BF16)


class Place:
    def __init__(self):
        d = lax.axis_index("dp")
        self.c, chip = d % PAIR, d // PAIR
        self.z, self.own = chip % LINE, chip // LINE
        x, y = self.own // PAIR, self.own % PAIR
        self.xs, self.ys, self.diag = (1 - x) * PAIR + y, x * PAIR + 1 - y, (1 - x) * PAIR + 1 - y
        self.near, self.far = pl.ds(self.z // PAIR * PAIR, PAIR), pl.ds(PAIR - self.z // PAIR * PAIR, PAIR)
        self.inner = jnp.logical_or(self.z == 1, self.z == 2)
        self.outer = jnp.logical_not(self.inner)
        at = lambda plane, z, c: {"dp": (plane * LINE + z) * PAIR + c}
        self.to_x, self.to_y, self.to_diag = (at(plane, self.z, self.c) for plane in (self.xs, self.ys, self.diag))
        self.to_c = at(self.own, self.z, 1 - self.c)
        self.to_z = [at(self.own, (self.z + k) % LINE, self.c) for k in range(1, LINE)]
        self.next_z = at(self.own, self.z + 1 - PAIR * (self.z % PAIR), self.c)
        self.across_z = at(self.own, LINE - 1 - self.z, self.c)
        self.sharers = [self.to_x, self.to_y, self.to_c, *self.to_z]


def signal_all(sem, devices):
    for device in devices:
        pl.semaphore_signal(sem, inc=1, device_id=device, device_id_type=MESH)


def greet(devices):
    barrier = pltpu.get_barrier_semaphore()
    signal_all(barrier, devices)
    pl.semaphore_wait(barrier, len(devices))


def send(src, dst, send_sem, recv_sem, device):
    pltpu.make_async_remote_copy(src, dst, send_sem, recv_sem, device_id=device, device_id_type=MESH).start()


def await_bytes(ref, sem):
    pltpu.make_async_copy(ref, ref, sem).wait()


class Gather:
    Z, Z2, Z3, XA, XB, YA, YB, DX, DY, C, OWN, SENT = SLOTS = range(12)

    def __init__(self, place, mine, blocks, amount, sems, direct):
        self.p, self.mine, self.blocks, self.amount, self.sems, self.direct = place, mine, blocks, amount, sems, direct

    def z_first(self):
        p = self.p
        (here,) = self.blocks(p.own, p.z, p.c)
        pltpu.make_async_copy(self.mine, here, self.sems.at[self.OWN]).start()
        for device in p.to_z if self.direct else [p.next_z]:
            send(self.mine, here, self.sems.at[self.SENT], self.sems.at[self.Z], device)

    def _move(self, plane, zs, slot, device):
        for ref in self.blocks(plane, zs, self.p.c):
            send(ref, ref, self.sems.at[self.SENT], self.sems.at[slot], device)

    def _wait(self, slot, blocks=PAIR):
        await_bytes(self.amount(blocks), self.sems.at[slot])

    def z_second(self):
        @pl.when(self.p.inner)
        def _():
            self._wait(self.Z, 1)
            self._wait(self.OWN, 1)
            self._move(self.p.own, self.p.near, self.Z2, self.p.across_z)

    def z_third(self):
        @pl.when(self.p.inner)
        def _():
            self._wait(self.Z2)
            self._move(self.p.own, self.p.far, self.Z3, self.p.next_z)

    def plane(self):
        p = self.p
        if self.direct:
            self._wait(self.Z, LINE - 1)
            self._wait(self.OWN, 1)
        else:

            @pl.when(p.outer)
            def _():
                self._wait(self.Z, 1)
                self._wait(self.OWN, 1)
                self._wait(self.Z3)

        self._move(p.own, LO, self.XA, p.to_x)
        self._move(p.own, HI, self.YB, p.to_y)
        self._move(p.own, HI, self.XB, p.to_x)
        self._move(p.own, LO, self.YA, p.to_y)
        self._move(p.own, ALL, self.C, p.to_c)

    def across(self):
        p = self.p
        self._wait(self.XA)
        self._move(p.xs, LO, self.DY, p.to_y)
        self._wait(self.YB)
        self._move(p.ys, HI, self.DX, p.to_x)

    def to_core(self):
        p = self.p
        self._wait(self.XB)
        self._move(p.xs, ALL, self.C, p.to_c)
        self._wait(self.YA)
        self._move(p.ys, ALL, self.C, p.to_c)

    def last_to_core(self):
        self._wait(self.DY)
        self._wait(self.DX)
        self._move(self.p.diag, ALL, self.C, self.p.to_c)

    def done(self):
        self._wait(self.C, PLANE * LINE)

    def sent(self):
        for _ in range(LINE - 1 if self.direct else 1):
            await_bytes(self.mine, self.sems.at[self.SENT])
        if not self.direct:
            pl.when(self.p.inner)(functools.partial(self._wait, self.SENT, LINE))
        for _ in range(7):
            self._wait(self.SENT, LINE)


def add_into(dst, *srcs):
    def one(i, _):
        for z in range(dst.shape[1]):
            total = srcs[0][i, z].astype(F32)
            for s in srcs[1:]:
                total += s[i, z].astype(F32)
            dst[i, z] = total.astype(dst.dtype)
        return 0

    if dst.shape[0] == 1:
        one(0, 0)
    else:
        lax.fori_loop(0, dst.shape[0], one, 0)


class Scatter:
    P1X, P1Y, XA, XB, YA, YB, Z, SENT, *C, L0, L1, L2, L3 = SLOTS = range(16)
    L = (L0, L1, L2, L3)

    @staticmethod
    def scratch(n, r, w):
        return [pltpu.VMEM(s + (r, w), BF16) for s in ((PLANE, n, LINE), (PLANE, n, LINE), (n, 3 * LINE), (LINE - 1, n))]

    def __init__(self, place, n, terms, out, slot, sems, acc):
        self.p, self.n, self.terms, self.out, self.sems, self.acc = place, n, terms, out, sems, acc
        mine, other, arrived, rz = slot
        some = pl.ds(0, n)
        self.mine, self.other = (lambda g, zs=ALL: mine.at[g, some, zs]), (lambda g, zs=ALL: other.at[g, some, zs])
        self.p1x, self.p1y = arrived.at[some, LO], arrived.at[some, HI]
        self.rx, self.ry = (lambda lo: arrived.at[some, pl.ds(LINE + lo, PAIR)]), (lambda lo: arrived.at[some, pl.ds(PAIR * LINE + lo, PAIR)])
        self.rz, self.kept = rz.at[:, some], mine

    def start(self):
        p = self.p
        for g, plane in enumerate((p.diag, p.xs, p.ys, p.own)):
            for ref, part in self.terms(plane, 1 - p.c):
                send(ref, part(self.other(g)), self.sems.at[self.SENT], self.sems.at[self.C[g]], p.to_c)
            for ref, part in self.terms(plane, p.c):
                pltpu.make_async_copy(ref, part(self.mine(g)), self.sems.at[self.L[g]]).start()

    def _both(self, g):
        await_bytes(self.other(g), self.sems.at[self.C[g]])
        await_bytes(self.mine(g), self.sems.at[self.L[g]])

    def _send(self, src, dst, slot, device):
        send(src, dst, self.sems.at[self.SENT], self.sems.at[slot], device)

    def diagonal(self):
        p = self.p
        self._both(0)
        add_into(self.mine(0), self.mine(0), self.other(0))
        self._send(self.mine(0, LO), self.p1x, self.P1X, p.to_x)
        self._send(self.mine(0, HI), self.p1y, self.P1Y, p.to_y)

    def straight(self):
        p = self.p
        self._both(1)
        add_into(self.mine(1, LO), self.mine(1, LO), self.other(1, LO))
        self._send(self.mine(1, LO), self.rx(0), self.XA, p.to_x)
        self._both(2)
        add_into(self.mine(2, HI), self.mine(2, HI), self.other(2, HI))
        self._send(self.mine(2, HI), self.ry(PAIR), self.YB, p.to_y)

    def joined(self):
        p = self.p
        await_bytes(self.p1y, self.sems.at[self.P1Y])
        add_into(self.mine(1, HI), self.mine(1, HI), self.other(1, HI), self.p1y)
        self._send(self.mine(1, HI), self.rx(PAIR), self.XB, p.to_x)
        await_bytes(self.p1x, self.sems.at[self.P1X])
        add_into(self.mine(2, LO), self.mine(2, LO), self.other(2, LO), self.p1x)
        self._send(self.mine(2, LO), self.ry(0), self.YA, p.to_y)

    def along_z(self):
        p = self.p
        self._both(3)
        for part, lo, xs, ys in ((LO, 0, self.XA, self.YA), (HI, PAIR, self.XB, self.YB)):
            await_bytes(self.rx(lo), self.sems.at[xs])
            await_bytes(self.ry(lo), self.sems.at[ys])
            add_into(self.mine(3, part), self.mine(3, part), self.other(3, part), self.rx(lo), self.ry(lo))
        for k, device in enumerate(p.to_z):
            self._send(self.mine(3, (p.z + 1 + k) % LINE), self.rz.at[k], self.Z, device)

    def last(self):
        await_bytes(self.rz, self.sems.at[self.Z])
        for i in range(self.n):
            total = self.kept[3, i, self.p.z].astype(F32)
            for k in range(LINE - 1):
                total += self.rz[k, i].astype(F32)
            g = total.astype(BF16)
            self.out(i)[:] = g
            g = g.astype(F32)
            g = g * g
            r, w = g.shape
            lanes = g[:, :LANES]
            for k in range(1, w // LANES):
                lanes += g[:, LANES * k : LANES * (k + 1)]
            self.acc[:] += jnp.sum(lanes.reshape(-1, *self.acc.shape), 0)

    def sent(self):
        for _ in range(7):
            await_bytes(self.other(0), self.sems.at[self.SENT])
        await_bytes(self.rz, self.sems.at[self.SENT])


class Pump:
    def __init__(self):
        self.items, self.now = [], 0.0

    def insert(self, when, act, tag=None):
        at = len(self.items)
        while at and self.items[at - 1][0] > when:
            at -= 1
        self.items.insert(at, (when, act, tag))

    def due(self):
        acts = []
        while self.items and self.items[0][0] <= self.now:
            acts.append(self.items.pop(0)[1])
        return acts

    def through(self, tag):
        acts = []
        while any(t == tag for _, _, t in self.items):
            when, act, _ = self.items.pop(0)
            self.now = max(self.now, when)
            acts.append(act)
        return acts

    def plan(self, steps, cost, gates=None, inject=None):
        ticks = {}
        for s in range(steps):
            self.now += cost
            if inject and s in inject:
                for put in inject[s]:
                    put()
            acts = self.due()
            if gates and s + 1 in gates:
                acts += self.through(gates[s + 1])
            if acts:
                ticks[s] = acts
        return ticks


def run(acts):
    for act in acts:
        act()


def stream(steps, ins, outs, body, ticks, late=(), before=None):
    def fetch(step):
        for where, buf, sem in ins:
            pltpu.make_async_copy(where(step), buf.at[step % PAIR], sem.at[step % PAIR]).start()

    def one(step, _):
        slot = step % PAIR
        early = step + 1 < steps
        for t in late:
            early = jnp.logical_and(early, step != t)
        pl.when(early)(lambda: fetch(step + 1))
        for _, buf, sem in ins:
            await_bytes(buf.at[slot], sem.at[slot])
        body(step, [buf.at[slot] for _, buf, _ in ins], [buf.at[slot] for _, buf, _ in outs])

        @pl.when(step >= 1)
        def _():
            for _, buf, sem in outs:
                await_bytes(buf.at[1 - slot], sem.at[1 - slot])

        for where, buf, sem in outs:
            pltpu.make_async_copy(buf.at[slot], where(step), sem.at[slot]).start()
        for t, acts in plan.items():
            pl.when(step == t)(functools.partial(run, acts))
        for t in late:
            pl.when(step == t)(lambda t=t: fetch(t + 1))
        return 0

    fetch(0)
    if before is not None:
        before()
    plan = ticks()
    lax.fori_loop(0, steps, one, 0)
    for _, buf, sem in outs:
        await_bytes(buf.at[(steps - 1) % PAIR], sem.at[(steps - 1) % PAIR])


def cols(step, width):
    return pl.ds(pl.multiple_of(step * width, width), width)


def cuts(total, *shares):
    whole, at, parts = sum(shares), 0, []
    for k in range(len(shares)):
        end = -(-total * sum(shares[: k + 1]) // whole)
        if end > at:
            parts.append((at, end - at))
        at = end
    return parts


def concat(ref, n):
    return jnp.concatenate([ref[j] for j in range(n)], axis=-1)


shape = jax.ShapeDtypeStruct
any_, whole = pl.BlockSpec(memory_space=pl.ANY), pl.BlockSpec(memory_space=pltpu.VMEM)


def two(*dims, dtype=BF16):
    return pltpu.VMEM((PAIR, *dims), dtype)


class Sizes:
    def __init__(self, tokens, d, ff):
        self.tokens, self.d, self.ff, self.half = tokens, d, ff, d // PAIR
        self.tiles, self.rd, self.rf = ff // TILE, d // DEVICES, ff // DEVICES
        self.parts = cuts(self.tiles, *SHARES[1])
        self.deep, self.tall, self.wide = (self.tiles, *GRID, self.rd, TILE), (ff, d), (self.tiles, tokens, TILE)
        self.thin, self.turned = (tokens, d), (d, tokens)
        self.blocks = [shape((self.rd, ff), BF16)] * PAIR + [shape((self.rf, d), BF16)]
        slots = Scatter.scratch(1, self.rf, self.half) * PAIR
        for _, size in self.parts:
            slots += Scatter.scratch(size, self.rd, TILE) * PAIR
        self.n_slots = PAIR + PAIR * len(self.parts)
        self.slot_size, self.slots = len(slots) // self.n_slots, slots
        many = PAIR if tokens % (PAIR * LINE * TILE) == 0 else 1
        self.halves = [pl.ds(q * (tokens // many), tokens // many) for q in range(many)]
        self.hidden_bufs = [two(tokens, TILE, dtype=F32)] * PAIR + [two(TILE, d)] + [two(tokens, TILE)] * PAIR
        self.hidden_bufs += [two(*GRID, self.rd, TILE)] * PAIR + [two(TILE, d)]


def block_rows(plane, z, c, r):
    return pl.ds(pl.multiple_of(((plane * LINE + z) * PAIR + c) * r, 8), r)


def piece(refs, bufs, sems):
    return [(lambda s, ref=ref: ref.at[s], buf, sems.at[k]) for k, (ref, buf) in enumerate(zip(refs, bufs, strict=True))]


def scatters(place, pump, size, slots, sems, acc, out, down, wide):
    state = {"free": 0.0}

    def scatter(n, terms, to, slot, share):
        one = Scatter(place, n, terms, to, slots[slot], sems.at[slot], acc)
        wire = WIRE * share

        def put():
            now = pump.now
            start = max(now + 3, state["free"])
            state["free"] = start + wire
            ahead, end = max(now + 3, start - 4), start + 1.6 * wire + 5
            acts = [(now, one.start), (ahead, one.diagonal), (ahead, one.straight), (start + 0.4 * wire, one.joined)]
            acts += [(start + wire + 2, one.along_z), (end, one.last), (end, one.sent)]
            for when, act in acts:
                pump.insert(when, act)

        return put

    def down_job(k):
        part = pl.ds(k * size.half, size.half)
        terms = lambda plane, c: [(down.at[block_rows(plane, z, c, size.rf), part], lambda to, z=z: to.at[0, z]) for z in range(LINE)]
        return scatter(1, terms, lambda i: out[-1].at[:, part], k, 0.5)

    def wide_job(b, k):
        start, n = size.parts[b]
        terms = lambda plane, c: [(wide[k].at[pl.ds(start, n), plane, :, c], lambda to: to)]
        to = lambda i: out[k].at[:, pl.ds((start + i) * TILE, TILE)]
        return scatter(n, terms, to, PAIR + PAIR * b + k, n / size.tiles)

    jobs = [[down_job(k) for k in range(PAIR)]] + [[wide_job(b, k) for k in range(PAIR)] for b in range(len(size.parts))]

    def put_all(puts):
        for put in puts:
            put()

    return [functools.partial(put_all, puts) for puts in jobs]


def hidden(size, pump, by, at, ins, grads, kept, puts, cost, before, sems, gbuf, ubuf, wdbuf, dgbuf, dubuf, gout, uout, wbuf):
    in_sem, out_sem = sems
    gate, up, w_down = ins

    def body(step, ins, outs):
        dg, du = outs[PAIR:] if kept else (dgbuf.at[0], dubuf.at[0])
        for part in size.halves:
            by_act = nt(by[part, :], ins[2][:]).astype(BF16).astype(F32)
            dg[part, :], du[part, :] = silu_back(ins[0][part, :], ins[1][part, :], by_act)
        for out, grad in zip(outs, (dg, du)):
            out[:] = nn(at[:], grad[:]).astype(BF16).reshape(*GRID, size.rd, TILE)

    outs = piece((*grads, *kept), (gout, uout, dgbuf, dubuf)[: PAIR + len(kept)], out_sem)
    inject = {min(start + n, size.tiles - 1): [put] for (start, n), put in zip(size.parts, puts[:-1])}
    streams = piece((gate, up), (gbuf, ubuf), in_sem)
    streams.append((lambda s: w_down.at[cols(s, TILE), :], wdbuf, in_sem.at[2]))
    before = before and functools.partial(before, dgbuf, wbuf)
    stream(size.tiles, streams, outs, body, lambda: pump.plan(size.tiles, cost, inject=inject), before=before)
    puts[-1]()
    run(pump.due())


def first_part(x, dy, weights):
    size = Sizes(*x.shape, weights[0].shape[-1])
    tokens, d, ff, tiles, rd, rf, half = size.tokens, size.d, size.ff, size.tiles, size.rd, size.rf, size.half
    rows, few = tokens // LINE, tokens // (PAIR * LINE)
    chunks = [cuts(tiles, *shares) for shares in SHARES[0]]
    jobs_of, gates = [], [{}, {}]
    for layer in range(PAIR):
        for start, n in chunks[layer]:
            if layer and start == chunks[1][-1][0]:
                jobs_of.append((1, 2, 0, half))
            jobs_of += [(layer, 0, start, n), (layer, 1, start, n)]
            gates[layer][start] = len(jobs_of) - 1
        jobs_of += [(1, 2, half, half)] if layer else [(0, 2, 0, half), (0, 2, half, half)]
        gates[layer]["down"] = len(jobs_of) - 1
    nj = len(jobs_of)
    held_shapes = [(PAIR, tiles, rd, TILE), (PAIR, tiles, rd, TILE), (PAIR, rf, d)]
    deep, tall, wide, thin, turned = size.deep, size.tall, size.wide, size.thin, size.turned
    hbm = [turned, wide, deep, deep, tall, deep, deep, tall, thin, tall, wide, wide, deep, deep]
    hbm = [shape(thin, BF16), shape(tall, BF16), shape(wide, F32), shape(wide, F32)] + [shape(dims, BF16) for dims in hbm]
    hbm += [shape(wide, F32)] * PAIR
    scratch = [pltpu.VMEM(dims, BF16) for dims in held_shapes + [thin, thin, turned, deep]]

    def kernel(*refs):
        it = iter(refs)
        take = lambda n: [next(it) for _ in range(n)]
        x_hbm, dy_hbm, *w_hbm = take(PAIR + len(weights))
        *out, acc = take(len(weights) + 1)
        dh1, _, gate0, up0, a0t, act0, g0, u0, d0, g1, u1, d1, h1_hbm, dwd1, dg1, du1, dwg1, dwu1, gate1, up1 = take(len(hbm))
        full = [[g0, u0, d0], [g1, u1, d1]]
        *held, a, by, at, wg = take(len(scratch))
        slots = [take(size.slot_size) for _ in range(size.n_slots)]
        load_sem, ag_sems, rs_sems, in_sem, out_sem, one_sem = take(6)
        s_x, s_at, s_w, s_u = (one_sem.at[k] for k in range(4))
        place = Place()

        def load(k, layer):
            ref, sem = w_hbm[k].at[layer], load_sem.at[k, layer]
            if k == PAIR:
                pltpu.make_async_copy(ref, held[k].at[layer], sem).start()
            else:
                for t in range(tiles):
                    pltpu.make_async_copy(ref.at[:, pl.ds(TILE * t, TILE)], held[k].at[layer, t], sem).start()

        x_load = pltpu.make_async_copy(x_hbm, by, s_x)
        for layer in range(PAIR):
            for k in range(len(held)):
                load(k, layer)
                if k == 1 and not layer:
                    x_load.start()
        greet(place.sharers)
        acc[:] = jnp.zeros_like(acc)
        pump, jobs, loaded = Pump(), [], set()

        def first(j):
            layer, k, _, _ = jobs_of[j]
            if (k, layer) not in loaded:
                await_bytes(held[k].at[layer], load_sem.at[k, layer])
                loaded.add((k, layer))
            jobs[j].z_first()

        clock = begun = 4.0
        for j, (layer, k, start, n) in enumerate(jobs_of):
            part, ref = pl.ds(start, n), full[layer][k]
            if k == PAIR:

                def blocks(plane, zs, c, ref=ref, part=part):
                    zs = [zs.start + i for i in range(zs.size)] if isinstance(zs, pl.Slice) else [zs]
                    return [ref.at[block_rows(plane, z, c, rf), part] for z in zs]

                amount = lambda n, ref=ref, part=part: ref.at[pl.ds(0, n * rf), part]
                mine = held[k].at[layer, :, part]
            else:
                blocks = lambda plane, zs, c, ref=ref, part=part: [ref.at[part, plane, zs, c]]
                amount = lambda n, ref=ref, part=part: ref.at[part, pl.ds(0, max(1, n // LINE)), pl.ds(0, min(n, LINE)), 0]
                mine = held[k].at[layer, part]
            job = Gather(place, mine, blocks, amount, ag_sems.at[j], j < PAIR)
            jobs.append(job)
            took = TOOK * n / (d if k == PAIR else tiles)
            unit = took / 6
            lead = min(max(0.33 * clock - 5, 3), LEAD)
            zero = begun - 4
            pump.insert(zero, functools.partial(first, j))
            if not job.direct:
                pump.insert(zero + unit + 2.5, job.z_second)
                pump.insert(zero + 3 * unit + 5, job.z_third)
            ready = max(zero + 5 * unit + (5 if job.direct else 7.5), clock - lead)
            clock = max(clock, ready)
            pump.insert(ready, job.plane)
            pump.insert(clock + 0.4 * took, job.across)
            pump.insert(clock + 0.75 * took, job.to_core)
            behind = PAIR if j >= nj - 3 else lead
            pump.insert(clock + took + behind + 1, job.last_to_core)
            pump.insert(clock + took + behind + 2, job.done, j)
            clock += took
            begun += (0.5 if j > 1 else 0.2) * took
        pump.now = 3.0
        run(pump.due())
        x_load.wait()
        a0_out = pltpu.make_async_copy(at, a0t, s_at)
        dy_load = pltpu.make_async_copy(dy_hbm, by, s_x)

        step = min(TILE, tokens)

        def norm(i, _):
            part = cols(i, step)
            normed = norm_rows(by[part, :])
            a[part, :] = normed
            at[:, part] = normed.T
            return 0

        lax.fori_loop(0, tokens // step, norm, 0)
        a0_out.start()
        pump.now = 8.0

        def gate_up(layer, gate, up, before, wgate, wup, gbuf, ubuf, actbuf, dwbuf):
            def body(step, ins, outs):
                g = nn(a[:], ins[0][:].reshape(d, TILE))
                u = nn(a[:], ins[1][:].reshape(d, TILE))
                outs[0][:] = g
                outs[1][:] = u
                product = (g * jax.nn.sigmoid(g) * u).astype(BF16)
                if layer:
                    actbuf[0] = product
                    outs[2][:] = tn(actbuf[0], by[:]).astype(BF16)
                else:
                    outs[2][:] = product

            run(pump.through(gates[layer][0]))
            later = {s: j for s, j in gates[layer].items() if s in range(1, tiles)}
            outs = piece((gate, up, act0), (gbuf, ubuf, actbuf), out_sem)
            if layer:
                outs[-1] = (lambda s: dwd1.at[cols(s, TILE), :], dwbuf, out_sem.at[2])
            stream(
                tiles,
                piece(full[layer][:PAIR], (wgate, wup), in_sem),
                outs,
                body,
                lambda: pump.plan(tiles, 3.7 if layer else 2.5, later),
                late=[s - 1 for s in later],
                before=before,
            )

        def down(wd, tall, hbuf):
            run(pump.through(gates[0]["down"]))
            wd_load = pltpu.make_async_copy(d0, wd, s_w)
            wd_load.start()

            def ready():
                a0_out.wait()
                wd_load.wait()

            def body(step, ins, outs):
                part = cols(step, rows)
                h = by[part, :] + nn(concat(ins[0], tiles), wd[:]).astype(BF16)
                outs[0][:] = h
                normed = norm_rows(h)
                a[part, :] = normed
                at[:, part] = normed.T

            stream(
                tokens // rows,
                [(lambda s: act0.at[:, cols(s, rows), :], tall, in_sem.at[0])],
                [(lambda s: h1_hbm.at[cols(s, rows), :], hbuf, out_sem.at[0])],
                body,
                lambda: pump.plan(tokens // rows, 3.8),
                before=ready,
            )
            dy_load.start()

        tile_bufs = [two(*GRID, rd, TILE)] * PAIR + [two(tokens, TILE, dtype=F32)] * PAIR + [two(tokens, TILE), two(TILE, d)]
        pl.run_scoped(functools.partial(gate_up, 0, gate0, up0, None), *tile_bufs)
        pl.run_scoped(down, pltpu.VMEM(d0.shape, BF16), two(tiles, rows, TILE), two(rows, d))
        pl.run_scoped(functools.partial(gate_up, 1, gate1, up1, dy_load.wait), *tile_bufs)
        run(pump.through(nj - 1))
        assert not pump.items
        put_down, *put_wide = scatters(place, pump, size, slots, rs_sems, acc, out, dwd1, (dwg1, dwu1))
        put_down()
        run(pump.due())
        wg_load = pltpu.make_async_copy(g1, wg, s_w)
        wg_load.start()
        ins, grads = (gate1, up1, d1), (dwg1, dwu1)
        pl.run_scoped(
            functools.partial(hidden, size, pump, by, at, ins, grads, (dg1, du1), put_wide, 4.4, None, (in_sem, out_sem)), *size.hidden_bufs
        )

        def states(wu, dgbuf, dubuf, hbuf):
            wu_load = pltpu.make_async_copy(u1, wu, s_u)
            wu_load.start()

            def ready():
                wg_load.wait()
                wu_load.wait()

            def body(step, ins, outs):
                part = cols(step, few)
                dg, du, h = (ref for ref in ins)
                da = nt(concat(dg, tiles), concat(wg, tiles).reshape(d, ff)) + nt(concat(du, tiles), concat(wu, tiles).reshape(d, ff))
                by[part, :] = by[part, :] + norm_back(da.astype(BF16), h[:])

            ins = [(lambda s, ref=ref: ref.at[:, cols(s, few), :], buf, in_sem.at[k]) for k, (ref, buf) in enumerate(((dg1, dgbuf), (du1, dubuf)))]
            ins.append((lambda s: h1_hbm.at[cols(s, few), :], hbuf, in_sem.at[2]))
            stream(tokens // few, ins, [], body, lambda: pump.plan(tokens // few, 3.6), before=ready)

        pl.run_scoped(states, pltpu.VMEM(wg.shape, BF16), two(tiles, few, TILE), two(tiles, few, TILE), two(few, d))
        by_out = pltpu.make_async_copy(by, dh1, s_x)
        by_out.start()
        pump.now = 1e9
        run(pump.due())
        for job in jobs:
            job.sent()
        by_out.wait()

    DMA = pltpu.SemaphoreType.DMA
    outs = pl.pallas_call(
        kernel,
        name="first_part",
        in_specs=[any_] * (PAIR + len(weights)),
        out_specs=[whole] * (len(weights) + 1) + [any_] * len(hbm),
        out_shape=size.blocks + [shape((8, LANES), F32)] + hbm,
        scratch_shapes=scratch
        + size.slots
        + [DMA((3, PAIR)), DMA((nj, len(Gather.SLOTS))), DMA((size.n_slots, len(Scatter.SLOTS)))]
        + [DMA((4, PAIR)), DMA((4, PAIR)), DMA((4,))],
        compiler_params=pltpu.CompilerParams(collective_id=0, has_side_effects=True, vmem_limit_bytes=66_500_000),
    )(x, dy, *weights)
    *sums, acc = outs[: len(weights) + 1]
    dh1, _, gate0, up0, a0t, act0, _, _, d0 = outs[len(weights) + 1 :][:9]
    return sums, acc, (dh1, gate0, up0, a0t, act0, d0)


def second_part(last_acc, dh1, gate0, up0, a0t, act0, d0):
    size = Sizes(*dh1.shape, d0.shape[0])
    deep, tall = shape(size.deep, BF16), shape(size.tall, BF16)
    n = len(size.blocks)

    def kernel(*refs):
        it = iter(refs)
        take = lambda n: [next(it) for _ in range(n)]
        acc_in, dh1_hbm, gate0, up0, a0t, act0, d0 = take(7)
        *out, squares = take(n + 1)
        dwd0, dwg0, dwu0 = take(n)
        by, at = take(PAIR)
        slots = [take(size.slot_size) for _ in range(size.n_slots)]
        acc, sums, gone, rs_sems, in_sem, out_sem, sums_sem, one_sem = take(8)
        place, pump = Place(), Pump()
        by_load, at_load = pltpu.make_async_copy(dh1_hbm, by, one_sem.at[0]), pltpu.make_async_copy(a0t, at, one_sem.at[1])
        by_load.start()

        def between(abuf, wbuf):
            at_load.start()

            def ready():
                greet(place.sharers)
                acc[:] = acc_in[:]
                by_load.wait()

            def body(step, ins, outs):
                outs[0][:] = tn(ins[0][:], by[:]).astype(BF16)

            outs = [(lambda s: dwd0.at[cols(s, TILE), :], wbuf, out_sem.at[3])]
            stream(size.tiles, piece((act0,), (abuf,), in_sem.at[pl.ds(3, 1)]), outs, body, dict, before=ready)
            put_down()
            run(pump.due())
            at_load.wait()

        put_down, *put_wide = scatters(place, pump, size, slots, rs_sems, acc, out, dwd0, (dwg0, dwu0))
        ins, grads = (gate0, up0, d0), (dwg0, dwu0)
        pl.run_scoped(
            functools.partial(hidden, size, pump, by, at, ins, grads, (), put_wide, 3.9, between, (in_sem, out_sem)), *size.hidden_bufs
        )
        pump.now = 1e9
        run(pump.due())
        sums[0] = jnp.full(acc.shape, jnp.sum(acc[:]), F32)
        hops = [[place.to_c], [place.to_x, place.to_y, place.to_diag], place.to_z]
        at_gone = 0
        for k, devices in enumerate(hops):
            for i, device in enumerate(devices):
                send(sums.at[k], gone.at[at_gone + i], sums_sem.at[len(hops)], sums_sem.at[k], device)
            await_bytes(gone.at[pl.ds(at_gone, len(devices))], sums_sem.at[k])
            total = sums[k]
            for i in range(len(devices)):
                total += gone[at_gone + i]
            at_gone += len(devices)
            if k < len(hops) - 1:
                sums[k + 1] = total
            else:
                squares[:] = total
        await_bytes(gone, sums_sem.at[len(hops)])

    DMA = pltpu.SemaphoreType.DMA
    tile = (8, LANES)
    *sums, squares = pl.pallas_call(
        kernel,
        name="second_part",
        in_specs=[whole] + [any_] * 6,
        out_specs=[whole] * (n + 1) + [any_] * n,
        out_shape=size.blocks + [shape(tile, F32)] + [tall, deep, deep],
        scratch_shapes=[pltpu.VMEM(size.thin, BF16), pltpu.VMEM(size.turned, BF16)]
        + size.slots
        + [pltpu.VMEM(tile, F32), pltpu.VMEM((3, *tile), F32), pltpu.VMEM((7, *tile), F32)]
        + [DMA((size.n_slots, len(Scatter.SLOTS))), DMA((4, PAIR)), DMA((4, PAIR)), DMA((4,)), DMA((PAIR,))],
        compiler_params=pltpu.CompilerParams(collective_id=1, has_side_effects=True, vmem_limit_bytes=66_500_000),
    )(last_acc, dh1, gate0, up0, a0t, act0, d0)[: n + 1]
    return sums, squares


def adamw(weights, m, v, sums, squares):
    n = len(weights)
    count = DEVICES * sum(w.size for w in weights)

    def kernel(squares_ref, *refs):
        factor = jnp.minimum(1.0, 0.5 * lax.rsqrt(squares_ref[:1, :1] / count + 1e-30))
        for k in range(n):
            w, m, v, g, last_g, new_w, new_m, new_v = refs[k::n]
            grad = jnp.where(pl.program_id(0) == 0, g[:].astype(F32), last_g[:].astype(F32)) * factor
            m_next = 0.9 * m[0] + 0.1 * grad
            v_next = 0.95 * v[0] + 0.05 * grad * grad
            wide = w[0].astype(F32)
            new_w[0] = (wide - 0.02 * (m_next * lax.rsqrt(v_next + 1e-8) + 0.1 * wide)).astype(BF16)
            new_m[0] = m_next
            new_v[0] = v_next

    blocks = [pl.BlockSpec((1, *w.shape[1:]), lambda layer: (layer, 0, 0)) for w in weights]
    once = [pl.BlockSpec(s.shape, lambda layer: (0, 0)) for s in (squares, *sums)]
    return pl.pallas_call(
        kernel,
        name="adamw",
        grid=(PAIR,),
        in_specs=once[:1] + blocks * 3 + once[1:],
        out_specs=blocks * 3,
        out_shape=[shape(w.shape, BF16) for w in weights] + [shape(w.shape, F32) for w in weights] * PAIR,
    )(squares, *weights, *m, *v, *sums)


def solution(mesh):
    def step(x, dy, *arrays):
        weights, m, v = (arrays[3 * i : 3 * i + 3] for i in range(3))
        last, acc, kept = first_part(x[0], dy[0], weights)
        sums, squares = second_part(acc, *kept)
        return tuple(adamw(weights, m, v, [*sums, *last], squares))

    states, cut = P(("rep", "dp"), None, None), P(None, "dp", None)
    return jax.shard_map(
        step,
        mesh=mesh,
        in_specs=(states, states) + (cut,) * 9,
        out_specs=(P("rep", "dp", None),) * 9,
        check_vma=False,
    )
```

time: 1460 us -> 410 us (0.28)
  waiting for transfers between devices: 1030 us -> 0 us
  Pallas kernels: 0 us -> 408 us
  matrix products: 331 us -> 0 us
  blocking collectives: 36.8 us -> 0 us
  local copies, waits for them, and re-layouts: 20.4 us -> 0 us
  other arithmetic: 18.5 us -> 0 us
  between operations: 17.5 us -> 0.84 us
    reduce_scatter x6 -> x0, waiting for transfers between devices: 733 us -> none  [step(): lax.psum_scatter(by_w[name], 'dp', scatter_dimension=0, tiled=True)]
    pallas_call x0 -> x3, Pallas kernels: none -> 408 us  [the longest x1 283 us: first_part(): pl.pallas_call(kernel, name='first_part', in_specs=[any_] * (PAIR + len(w...]
    dot_general x15 -> x0, matrix products: 331 us -> none  [the longest x5 119 us: layer(): gate = jnp.dot(a, w['w_gate'], preferred_element_type=jnp.float32)]
    all_gather x6 -> x0, waiting for transfers between devices: 293 us -> none  [fetched(): lax.all_gather(w[number], 'dp', axis=0, tiled=True)]
    psum x1 -> x0, blocking collectives: 36.8 us -> none  [step(): squares = lax.psum(sum((jnp.sum(g * g) for g in gradients)), 'dp')]
    unnamed x32 -> x0, local copies, waits for them, and re-layouts: 15.1 us -> none
  transfers between devices with their start and end apart: 12 -> 0, of which waited for: 12 -> 0; matrix products, arithmetic and copies ran while one was open for 18% -> 0% of each run, Pallas kernels for 0% -> 0%
where the time goes in v2:
time: 410 us; the launch traced here: 409 us
  Pallas kernels  408 us (100%)
    pallas_call x1, Pallas kernels, first_part(): pl.pallas_call(kernel, name='first_part', in_specs=[any_] * (PAIR + len(w...  283 us
    pallas_call x1, Pallas kernels, second_part(): pl.pallas_call(kernel, name='second_part', in_specs=[whole] + [any_] * 6,...  120 us

profile of v2, /device:TPU:0, one launch (start us, length us, event | category | flops | bytes accessed | tf_op | source)
XLA Modules:
  0.0 409.1 jit_solution(9942317458404851852)
XLA Ops:
  0.6 282.6 %first_part.1 = (bf16[32,2816]{1,0:T(8,128)(2,1)}, bf16[32,2816]{1,0:T(8,128)(2,1)}, bf16[88,1024]{1,0:T(8,128)(2,1)}, f32[8,128]{1,0:T(8,128)}, bf16[2048,1024]...) custom-call(bf16[2048,1024]{1,0:T(8,128)(2,1)} %bitcast.2, ...), custom_call_target="tpu_custom_call" | custom-call | tf_op jit(solution)/shard_map/first_part/pallas_call | solution.py:685
  283.2 119.8 %second_part.1 = (bf16[32,2816]{1,0:T(8,128)(2,1)}, bf16[32,2816]{1,0:T(8,128)(2,1)}, bf16[88,1024]{1,0:T(8,128)(2,1)}, f32[8,128]{1,0:T(8,128)}, bf16[2816,1024...) custom-call(f32[8,128]{1,0:T(8,128)} %get-tuple-element.23.refs_0_, ...), custom_call_target="tpu_custom_call" | custom-call | tf_op jit(solution)/shard_map/second_part/pallas_call | solution.py:763
  403.1 5.9 %adamw.1 = (bf16[2,32,2816]{2,1,0:T(8,128)(2,1)}, bf16[2,32,2816]{2,1,0:T(8,128)(2,1)}, bf16[2,88,1024]{2,1,0:T(8,128)(2,1)}, f32[2,32,2816]{2,1,0:T(8,128)}, f3...) custom-call(f32[8,128]{1,0:T(8,128)} %get-tuple-element.30.squares_r, ...), custom_call_target="tpu_custom_call" | custom-call | tf_op jit(solution)/shard_map/adamw/pallas_call | solution.py:796

commit v3 on v2

--- a/solution.py
+++ b/solution.py
@@ -13,8 +13,10 @@
 PAIR = 2
 LO, HI, ALL = pl.ds(0, PAIR), pl.ds(PAIR, PAIR), pl.ds(0, LINE)
 GRID = (PLANE, LINE, PAIR)
-LEAD, TOOK, WIRE = 14, 24.0, 25.0
-SHARES = ((2, 4, 5), (3, 3, 3, 2)), (2, 3, 3, 3)
+LEAD, TOOK, WIRE, SLACK = 14, 24.0, 25.0, 99
+STATES, HID1, HID0 = 3.6, 4.4, 3.9
+DIRECT, PACE = 0.5, 0.5
+SHARES = ((3, 4, 4), (3, 3, 3, 2)), (2, 3, 3, 3)
 
 
 def nn(a, b):
@@ -76,7 +78,7 @@
 def greet(devices):
     barrier = pltpu.get_barrier_semaphore()
     signal_all(barrier, devices)
-    pl.semaphore_wait(barrier, len(devices))
+    return lambda: pl.semaphore_wait(barrier, len(devices))
 
 
 def send(src, dst, send_sem, recv_sem, device):
@@ -405,7 +407,7 @@
 
 
 def piece(refs, bufs, sems):
-    return [(lambda s, ref=ref: ref.at[s], buf, sems.at[k]) for k, (ref, buf) in enumerate(zip(refs, bufs, strict=True))]
+    return [(lambda s, ref=ref: ref.at[s], buf, sems.at[k]) for k, (ref, buf) in enumerate(zip(refs, bufs))]
 
 
 def scatters(place, pump, size, slots, sems, acc, out, down, wide):
@@ -417,7 +419,7 @@
 
         def put():
             now = pump.now
-            start = max(now + 3, state["free"])
+            start = max(now + 3, min(state["free"], now + SLACK * wire))
             state["free"] = start + wire
             ahead, end = max(now + 3, start - 4), start + 1.6 * wire + 5
             acts = [(now, one.start), (ahead, one.diagonal), (ahead, one.straight), (start + 0.4 * wire, one.joined)]
@@ -496,7 +498,7 @@
         take = lambda n: [next(it) for _ in range(n)]
         x_hbm, dy_hbm, *w_hbm = take(PAIR + len(weights))
         *out, acc = take(len(weights) + 1)
-        dh1, _, gate0, up0, a0t, act0, g0, u0, d0, g1, u1, d1, h1_hbm, dwd1, dg1, du1, dwg1, dwu1, gate1, up1 = take(len(hbm))
+        dh1, dwd0, gate0, up0, a0t, act0, g0, u0, d0, g1, u1, d1, h1_hbm, dwd1, dg1, du1, dwg1, dwu1, gate1, up1 = take(len(hbm))
         full = [[g0, u0, d0], [g1, u1, d1]]
         *held, a, by, at, wg = take(len(scratch))
         slots = [take(size.slot_size) for _ in range(size.n_slots)]
@@ -513,12 +515,13 @@
                     pltpu.make_async_copy(ref.at[:, pl.ds(TILE * t, TILE)], held[k].at[layer, t], sem).start()
 
         x_load = pltpu.make_async_copy(x_hbm, by, s_x)
+        greeting = greet(place.sharers)
         for layer in range(PAIR):
             for k in range(len(held)):
                 load(k, layer)
                 if k == 1 and not layer:
                     x_load.start()
-        greet(place.sharers)
+        greeting()
         acc[:] = jnp.zeros_like(acc)
         pump, jobs, loaded = Pump(), [], set()
 
@@ -563,7 +566,7 @@
             pump.insert(clock + took + behind + 1, job.last_to_core)
             pump.insert(clock + took + behind + 2, job.done, j)
             clock += took
-            begun += (0.5 if j > 1 else 0.2) * took
+            begun += (PACE if j > 1 else DIRECT) * took
         pump.now = 3.0
         run(pump.due())
         x_load.wait()
@@ -651,7 +654,7 @@
         wg_load.start()
         ins, grads = (gate1, up1, d1), (dwg1, dwu1)
         pl.run_scoped(
-            functools.partial(hidden, size, pump, by, at, ins, grads, (dg1, du1), put_wide, 4.4, None, (in_sem, out_sem)), *size.hidden_bufs
+            functools.partial(hidden, size, pump, by, at, ins, grads, (dg1, du1), put_wide, HID1, None, (in_sem, out_sem)), *size.hidden_bufs
         )
 
         def states(wu, dgbuf, dubuf, hbuf):
@@ -670,11 +673,20 @@
 
             ins = [(lambda s, ref=ref: ref.at[:, cols(s, few), :], buf, in_sem.at[k]) for k, (ref, buf) in enumerate(((dg1, dgbuf), (du1, dubuf)))]
             ins.append((lambda s: h1_hbm.at[cols(s, few), :], hbuf, in_sem.at[2]))
-            stream(tokens // few, ins, [], body, lambda: pump.plan(tokens // few, 3.6), before=ready)
+            stream(tokens // few, ins, [], body, lambda: pump.plan(tokens // few, STATES), before=ready)
 
         pl.run_scoped(states, pltpu.VMEM(wg.shape, BF16), two(tiles, few, TILE), two(tiles, few, TILE), two(few, d))
         by_out = pltpu.make_async_copy(by, dh1, s_x)
         by_out.start()
+
+        def down_gradient(abuf, wbuf):
+            def body(step, ins, outs):
+                outs[0][:] = tn(ins[0][:], by[:]).astype(BF16)
+
+            outs = [(lambda s: dwd0.at[cols(s, TILE), :], wbuf, out_sem.at[0])]
+            stream(tiles, piece((act0,), (abuf,), in_sem), outs, body, lambda: pump.plan(tiles, 1.4))
+
+        pl.run_scoped(down_gradient, two(tokens, TILE), two(TILE, d))
         pump.now = 1e9
         run(pump.due())
         for job in jobs:
@@ -695,49 +707,42 @@
         compiler_params=pltpu.CompilerParams(collective_id=0, has_side_effects=True, vmem_limit_bytes=66_500_000),
     )(x, dy, *weights)
     *sums, acc = outs[: len(weights) + 1]
-    dh1, _, gate0, up0, a0t, act0, _, _, d0 = outs[len(weights) + 1 :][:9]
-    return sums, acc, (dh1, gate0, up0, a0t, act0, d0)
-
-
-def second_part(last_acc, dh1, gate0, up0, a0t, act0, d0):
+    dh1, dwd0, gate0, up0, a0t, _, _, _, d0 = outs[len(weights) + 1 :][:9]
+    return sums, acc, (dh1, dwd0, gate0, up0, a0t, d0)
+
+
+def second_part(last_acc, dh1, dwd0, gate0, up0, a0t, d0):
     size = Sizes(*dh1.shape, d0.shape[0])
-    deep, tall = shape(size.deep, BF16), shape(size.tall, BF16)
+    deep = shape(size.deep, BF16)
     n = len(size.blocks)
 
     def kernel(*refs):
         it = iter(refs)
         take = lambda n: [next(it) for _ in range(n)]
-        acc_in, dh1_hbm, gate0, up0, a0t, act0, d0 = take(7)
+        acc_in, dh1_hbm, dwd0, gate0, up0, a0t, d0 = take(7)
         *out, squares = take(n + 1)
-        dwd0, dwg0, dwu0 = take(n)
+        dwg0, dwu0 = take(PAIR)
         by, at = take(PAIR)
         slots = [take(size.slot_size) for _ in range(size.n_slots)]
         acc, sums, gone, rs_sems, in_sem, out_sem, sums_sem, one_sem = take(8)
         place, pump = Place(), Pump()
         by_load, at_load = pltpu.make_async_copy(dh1_hbm, by, one_sem.at[0]), pltpu.make_async_copy(a0t, at, one_sem.at[1])
         by_load.start()
-
-        def between(abuf, wbuf):
-            at_load.start()
-
-            def ready():
-                greet(place.sharers)
-                acc[:] = acc_in[:]
-                by_load.wait()
-
-            def body(step, ins, outs):
-                outs[0][:] = tn(ins[0][:], by[:]).astype(BF16)
-
-            outs = [(lambda s: dwd0.at[cols(s, TILE), :], wbuf, out_sem.at[3])]
-            stream(size.tiles, piece((act0,), (abuf,), in_sem.at[pl.ds(3, 1)]), outs, body, dict, before=ready)
+        at_load.start()
+        greeting = greet(place.sharers + [place.to_diag])
+
+        def ready(*_):
+            greeting()
             put_down()
             run(pump.due())
+            acc[:] = acc_in[:]
+            by_load.wait()
             at_load.wait()
 
         put_down, *put_wide = scatters(place, pump, size, slots, rs_sems, acc, out, dwd0, (dwg0, dwu0))
         ins, grads = (gate0, up0, d0), (dwg0, dwu0)
         pl.run_scoped(
-            functools.partial(hidden, size, pump, by, at, ins, grads, (), put_wide, 3.9, between, (in_sem, out_sem)), *size.hidden_bufs
+            functools.partial(hidden, size, pump, by, at, ins, grads, (), put_wide, HID0, ready, (in_sem, out_sem)), *size.hidden_bufs
         )
         pump.now = 1e9
         run(pump.due())
@@ -764,14 +769,14 @@
         kernel,
         name="second_part",
         in_specs=[whole] + [any_] * 6,
-        out_specs=[whole] * (n + 1) + [any_] * n,
-        out_shape=size.blocks + [shape(tile, F32)] + [tall, deep, deep],
+        out_specs=[whole] * (n + 1) + [any_] * PAIR,
+        out_shape=size.blocks + [shape(tile, F32)] + [deep, deep],
         scratch_shapes=[pltpu.VMEM(size.thin, BF16), pltpu.VMEM(size.turned, BF16)]
         + size.slots
         + [pltpu.VMEM(tile, F32), pltpu.VMEM((3, *tile), F32), pltpu.VMEM((7, *tile), F32)]
         + [DMA((size.n_slots, len(Scatter.SLOTS))), DMA((4, PAIR)), DMA((4, PAIR)), DMA((4,)), DMA((PAIR,))],
         compiler_params=pltpu.CompilerParams(collective_id=1, has_side_effects=True, vmem_limit_bytes=66_500_000),
-    )(last_acc, dh1, gate0, up0, a0t, act0, d0)[: n + 1]
+    )(last_acc, dh1, dwd0, gate0, up0, a0t, d0)[: n + 1]
     return sums, squares
 
 

time: 410 us -> 395 us (0.963)
  Pallas kernels: 408 us -> 393 us
    pallas_call x1, Pallas kernels: 120 us -> 99.8 us  [second_part(): pl.pallas_call(kernel, name='second_part', in_specs=[whole] + [any_] * 6,...]
    pallas_call x1, Pallas kernels: 283 us -> 288 us  [first_part(): pl.pallas_call(kernel, name='first_part', in_specs=[any_] * (PAIR + len(w...]
where the time goes in v3:
time: 395 us; the launch traced here: 394 us
  Pallas kernels  393 us (99%)
    pallas_call x1, Pallas kernels, first_part(): pl.pallas_call(kernel, name='first_part', in_specs=[any_] * (PAIR + len(w...  288 us
    pallas_call x1, Pallas kernels, second_part(): pl.pallas_call(kernel, name='second_part', in_specs=[whole] + [any_] * 6,...  99.8 us

profile of v3, /device:TPU:0, one launch (start us, length us, event | category | flops | bytes accessed | tf_op | source)
XLA Modules:
  0.0 394.2 jit_solution(5576911773988636645)
XLA Ops:
  0.6 287.7 %first_part.1 = (bf16[32,2816]{1,0:T(8,128)(2,1)}, bf16[32,2816]{1,0:T(8,128)(2,1)}, bf16[88,1024]{1,0:T(8,128)(2,1)}, f32[8,128]{1,0:T(8,128)}, bf16[2048,1024]...) custom-call(bf16[2048,1024]{1,0:T(8,128)(2,1)} %bitcast.2, ...), custom_call_target="tpu_custom_call" | custom-call | tf_op jit(solution)/shard_map/first_part/pallas_call | solution.py:697
  288.4 99.8 %second_part.1 = (bf16[32,2816]{1,0:T(8,128)(2,1)}, bf16[32,2816]{1,0:T(8,128)(2,1)}, bf16[88,1024]{1,0:T(8,128)(2,1)}, f32[8,128]{1,0:T(8,128)}, bf16[11,4,4,2,...) custom-call(f32[8,128]{1,0:T(8,128)} %get-tuple-element.23.refs_0_, ...), custom_call_target="tpu_custom_call" | custom-call | tf_op jit(solution)/shard_map/second_part/pallas_call | solution.py:768
  388.2 5.9 %adamw.1 = (bf16[2,32,2816]{2,1,0:T(8,128)(2,1)}, bf16[2,32,2816]{2,1,0:T(8,128)(2,1)}, bf16[2,88,1024]{2,1,0:T(8,128)(2,1)}, f32[2,32,2816]{2,1,0:T(8,128)}, f3...) custom-call(f32[8,128]{1,0:T(8,128)} %get-tuple-element.30.squares_r, ...), custom_call_target="tpu_custom_call" | custom-call | tf_op jit(solution)/shard_map/adamw/pallas_call | solution.py:801

commit v4 on v3

--- a/solution.py
+++ b/solution.py
@@ -13,10 +13,11 @@
 PAIR = 2
 LO, HI, ALL = pl.ds(0, PAIR), pl.ds(PAIR, PAIR), pl.ds(0, LINE)
 GRID = (PLANE, LINE, PAIR)
-LEAD, TOOK, WIRE, SLACK = 14, 24.0, 25.0, 99
+LEAD, TOOK = 14, 24.0
+TEMPOS = (25.0, 4, 1.6), (25.0, 6, 1.6)
 STATES, HID1, HID0 = 3.6, 4.4, 3.9
 DIRECT, PACE = 0.5, 0.5
-SHARES = ((3, 4, 4), (3, 3, 3, 2)), (2, 3, 3, 3)
+SHARES = ((3, 4, 4), (3, 3, 3, 2)), (3, 3, 3, 2), (2, 3, 3, 3)
 
 
 def nn(a, b):
@@ -168,8 +169,8 @@
             await_bytes(self.mine, self.sems.at[self.SENT])
         if not self.direct:
             pl.when(self.p.inner)(functools.partial(self._wait, self.SENT, LINE))
-        for _ in range(7):
-            self._wait(self.SENT, LINE)
+        for blocks in (PLANE, PLANE - 1):
+            self._wait(self.SENT, blocks * LINE)
 
 
 def add_into(dst, *srcs):
@@ -384,10 +385,10 @@
 
 
 class Sizes:
-    def __init__(self, tokens, d, ff):
+    def __init__(self, shares, tokens, d, ff):
         self.tokens, self.d, self.ff, self.half = tokens, d, ff, d // PAIR
         self.tiles, self.rd, self.rf = ff // TILE, d // DEVICES, ff // DEVICES
-        self.parts = cuts(self.tiles, *SHARES[1])
+        self.parts = cuts(self.tiles, *shares)
         self.deep, self.tall, self.wide = (self.tiles, *GRID, self.rd, TILE), (ff, d), (self.tiles, tokens, TILE)
         self.thin, self.turned = (tokens, d), (d, tokens)
         self.blocks = [shape((self.rd, ff), BF16)] * PAIR + [shape((self.rf, d), BF16)]
@@ -399,7 +400,7 @@
         many = PAIR if tokens % (PAIR * LINE * TILE) == 0 else 1
         self.halves = [pl.ds(q * (tokens // many), tokens // many) for q in range(many)]
         self.hidden_bufs = [two(tokens, TILE, dtype=F32)] * PAIR + [two(TILE, d)] + [two(tokens, TILE)] * PAIR
-        self.hidden_bufs += [two(*GRID, self.rd, TILE)] * PAIR + [two(TILE, d)]
+        self.hidden_bufs += [two(*GRID, self.rd, TILE)] * PAIR
 
 
 def block_rows(plane, z, c, r):
@@ -410,18 +411,19 @@
     return [(lambda s, ref=ref: ref.at[s], buf, sems.at[k]) for k, (ref, buf) in enumerate(zip(refs, bufs))]
 
 
-def scatters(place, pump, size, slots, sems, acc, out, down, wide):
+def scatters(place, pump, size, slots, sems, acc, out, down, wide, tempo):
     state = {"free": 0.0}
 
     def scatter(n, terms, to, slot, share):
         one = Scatter(place, n, terms, to, slots[slot], sems.at[slot], acc)
-        wire = WIRE * share
+        matrix, head, tail = tempo
+        wire = matrix * share
 
         def put():
             now = pump.now
-            start = max(now + 3, min(state["free"], now + SLACK * wire))
+            start = max(now + 3, state["free"])
             state["free"] = start + wire
-            ahead, end = max(now + 3, start - 4), start + 1.6 * wire + 5
+            ahead, end = max(now + 3, start - head), start + tail * wire + 5
             acts = [(now, one.start), (ahead, one.diagonal), (ahead, one.straight), (start + 0.4 * wire, one.joined)]
             acts += [(start + wire + 2, one.along_z), (end, one.last), (end, one.sent)]
             for when, act in acts:
@@ -449,15 +451,17 @@
     return [functools.partial(put_all, puts) for puts in jobs]
 
 
-def hidden(size, pump, by, at, ins, grads, kept, puts, cost, before, sems, gbuf, ubuf, wdbuf, dgbuf, dubuf, gout, uout, wbuf):
+def hidden(size, pump, by, at, ins, grads, kept, held, puts, cost, before, sems, gbuf, ubuf, wdbuf, dgbuf, dubuf, gout, uout):
     in_sem, out_sem = sems
     gate, up, w_down = ins
+    dg, du = held or (dgbuf.at[0], dubuf.at[0])
 
     def body(step, ins, outs):
-        dg, du = outs[PAIR:] if kept else (dgbuf.at[0], dubuf.at[0])
         for part in size.halves:
             by_act = nt(by[part, :], ins[2][:]).astype(BF16).astype(F32)
-            dg[part, :], du[part, :] = silu_back(ins[0][part, :], ins[1][part, :], by_act)
+            dg[part, :], du[part, :] = both = silu_back(ins[0][part, :], ins[1][part, :], by_act)
+            for out, value in zip(outs[PAIR:], both):
+                out[part, :] = value
         for out, grad in zip(outs, (dg, du)):
             out[:] = nn(at[:], grad[:]).astype(BF16).reshape(*GRID, size.rd, TILE)
 
@@ -465,14 +469,13 @@
     inject = {min(start + n, size.tiles - 1): [put] for (start, n), put in zip(size.parts, puts[:-1])}
     streams = piece((gate, up), (gbuf, ubuf), in_sem)
     streams.append((lambda s: w_down.at[cols(s, TILE), :], wdbuf, in_sem.at[2]))
-    before = before and functools.partial(before, dgbuf, wbuf)
     stream(size.tiles, streams, outs, body, lambda: pump.plan(size.tiles, cost, inject=inject), before=before)
     puts[-1]()
     run(pump.due())
 
 
 def first_part(x, dy, weights):
-    size = Sizes(*x.shape, weights[0].shape[-1])
+    size = Sizes(SHARES[1], *x.shape, weights[0].shape[-1])
     tokens, d, ff, tiles, rd, rf, half = size.tokens, size.d, size.ff, size.tiles, size.rd, size.rf, size.half
     rows, few = tokens // LINE, tokens // (PAIR * LINE)
     chunks = [cuts(tiles, *shares) for shares in SHARES[0]]
@@ -647,14 +650,15 @@
         pl.run_scoped(functools.partial(gate_up, 1, gate1, up1, dy_load.wait), *tile_bufs)
         run(pump.through(nj - 1))
         assert not pump.items
-        put_down, *put_wide = scatters(place, pump, size, slots, rs_sems, acc, out, dwd1, (dwg1, dwu1))
+        put_down, *put_wide = scatters(place, pump, size, slots, rs_sems, acc, out, dwd1, (dwg1, dwu1), TEMPOS[0])
         put_down()
         run(pump.due())
         wg_load = pltpu.make_async_copy(g1, wg, s_w)
         wg_load.start()
         ins, grads = (gate1, up1, d1), (dwg1, dwu1)
+        room = [a.at[:, pl.ds(k * TILE, TILE)] for k in range(PAIR)]
         pl.run_scoped(
-            functools.partial(hidden, size, pump, by, at, ins, grads, (dg1, du1), put_wide, HID1, None, (in_sem, out_sem)), *size.hidden_bufs
+            functools.partial(hidden, size, pump, by, at, ins, grads, (dg1, du1), room, put_wide, HID1, None, (in_sem, out_sem)), *size.hidden_bufs
         )
 
         def states(wu, dgbuf, dubuf, hbuf):
@@ -712,7 +716,7 @@
 
 
 def second_part(last_acc, dh1, dwd0, gate0, up0, a0t, d0):
-    size = Sizes(*dh1.shape, d0.shape[0])
+    size = Sizes(SHARES[2], *dh1.shape, d0.shape[0])
     deep = shape(size.deep, BF16)
     n = len(size.blocks)
 
@@ -731,7 +735,7 @@
         at_load.start()
         greeting = greet(place.sharers + [place.to_diag])
 
-        def ready(*_):
+        def ready():
             greeting()
             put_down()
             run(pump.due())
@@ -739,10 +743,10 @@
             by_load.wait()
             at_load.wait()
 
-        put_down, *put_wide = scatters(place, pump, size, slots, rs_sems, acc, out, dwd0, (dwg0, dwu0))
+        put_down, *put_wide = scatters(place, pump, size, slots, rs_sems, acc, out, dwd0, (dwg0, dwu0), TEMPOS[1])
         ins, grads = (gate0, up0, d0), (dwg0, dwu0)
         pl.run_scoped(
-            functools.partial(hidden, size, pump, by, at, ins, grads, (), put_wide, HID0, ready, (in_sem, out_sem)), *size.hidden_bufs
+            functools.partial(hidden, size, pump, by, at, ins, grads, (), None, put_wide, HID0, ready, (in_sem, out_sem)), *size.hidden_bufs
         )
         pump.now = 1e9
         run(pump.due())

time: 395 us -> 390 us (0.987)
  Pallas kernels: 393 us -> 388 us
where the time goes in v4:
time: 390 us; the launch traced here: 389 us
  Pallas kernels  388 us (99%)
    pallas_call x1, Pallas kernels, first_part(): pl.pallas_call(kernel, name='first_part', in_specs=[any_] * (PAIR + len(w...  285 us
    pallas_call x1, Pallas kernels, second_part(): pl.pallas_call(kernel, name='second_part', in_specs=[whole] + [any_] * 6,...  97.7 us

profile of v4, /device:TPU:0, one launch (start us, length us, event | category | flops | bytes accessed | tf_op | source)
XLA Modules:
  0.0 389.0 jit_solution(4894828008249586150)
XLA Ops:
  0.6 284.6 %first_part.1 = (bf16[32,2816]{1,0:T(8,128)(2,1)}, bf16[32,2816]{1,0:T(8,128)(2,1)}, bf16[88,1024]{1,0:T(8,128)(2,1)}, f32[8,128]{1,0:T(8,128)}, bf16[2048,1024]...) custom-call(bf16[2048,1024]{1,0:T(8,128)(2,1)} %bitcast.2, ...), custom_call_target="tpu_custom_call" | custom-call | tf_op jit(solution)/shard_map/first_part/pallas_call | solution.py:701
  285.3 97.7 %second_part.1 = (bf16[32,2816]{1,0:T(8,128)(2,1)}, bf16[32,2816]{1,0:T(8,128)(2,1)}, bf16[88,1024]{1,0:T(8,128)(2,1)}, f32[8,128]{1,0:T(8,128)}, bf16[11,4,4,2,...) custom-call(f32[8,128]{1,0:T(8,128)} %get-tuple-element.23.refs_0_, ...), custom_call_target="tpu_custom_call" | custom-call | tf_op jit(solution)/shard_map/second_part/pallas_call | solution.py:772
  382.9 5.9 %adamw.1 = (bf16[2,32,2816]{2,1,0:T(8,128)(2,1)}, bf16[2,32,2816]{2,1,0:T(8,128)(2,1)}, bf16[2,88,1024]{2,1,0:T(8,128)(2,1)}, f32[2,32,2816]{2,1,0:T(8,128)}, f3...) custom-call(f32[8,128]{1,0:T(8,128)} %get-tuple-element.30.squares_r, ...), custom_call_target="tpu_custom_call" | custom-call | tf_op jit(solution)/shard_map/adamw/pallas_call | solution.py:805

commit v5 on v4

--- a/solution.py
+++ b/solution.py
@@ -400,7 +400,7 @@
         many = PAIR if tokens % (PAIR * LINE * TILE) == 0 else 1
         self.halves = [pl.ds(q * (tokens // many), tokens // many) for q in range(many)]
         self.hidden_bufs = [two(tokens, TILE, dtype=F32)] * PAIR + [two(TILE, d)] + [two(tokens, TILE)] * PAIR
-        self.hidden_bufs += [two(*GRID, self.rd, TILE)] * PAIR
+        self.hidden_bufs += [two(*GRID, self.rd, TILE)] * PAIR + [pltpu.VMEM((tokens, TILE), BF16)]
 
 
 def block_rows(plane, z, c, r):
@@ -451,10 +451,10 @@
     return [functools.partial(put_all, puts) for puts in jobs]
 
 
-def hidden(size, pump, by, at, ins, grads, kept, held, puts, cost, before, sems, gbuf, ubuf, wdbuf, dgbuf, dubuf, gout, uout):
+def hidden(size, pump, by, at, ins, grads, kept, held, puts, cost, before, sems, gbuf, ubuf, wdbuf, dgbuf, dubuf, gout, uout, own):
     in_sem, out_sem = sems
     gate, up, w_down = ins
-    dg, du = held or (dgbuf.at[0], dubuf.at[0])
+    dg, du = (own, *held) if held else (dgbuf.at[0], dubuf.at[0])
 
     def body(step, ins, outs):
         for part in size.halves:
@@ -656,7 +656,7 @@
         wg_load = pltpu.make_async_copy(g1, wg, s_w)
         wg_load.start()
         ins, grads = (gate1, up1, d1), (dwg1, dwu1)
-        room = [a.at[:, pl.ds(k * TILE, TILE)] for k in range(PAIR)]
+        room = [a.at[:, pl.ds(0, TILE)]]
         pl.run_scoped(
             functools.partial(hidden, size, pump, by, at, ins, grads, (dg1, du1), room, put_wide, HID1, None, (in_sem, out_sem)), *size.hidden_bufs
         )

time: 390 us -> 386 us (0.990)
  Pallas kernels: 388 us -> 384 us
where the time goes in v5:
time: 386 us; the launch traced here: 385 us
  Pallas kernels  384 us (99%)
    pallas_call x1, Pallas kernels, first_part(): pl.pallas_call(kernel, name='first_part', in_specs=[any_] * (PAIR + len(w...  281 us
    pallas_call x1, Pallas kernels, second_part(): pl.pallas_call(kernel, name='second_part', in_specs=[whole] + [any_] * 6,...  97.1 us

profile of v5, /device:TPU:0, one launch (start us, length us, event | category | flops | bytes accessed | tf_op | source)
XLA Modules:
  0.0 385.0 jit_solution(11662758180756417342)
XLA Ops:
  0.6 281.2 %first_part.1 = (bf16[32,2816]{1,0:T(8,128)(2,1)}, bf16[32,2816]{1,0:T(8,128)(2,1)}, bf16[88,1024]{1,0:T(8,128)(2,1)}, f32[8,128]{1,0:T(8,128)}, bf16[2048,1024]...) custom-call(bf16[2048,1024]{1,0:T(8,128)(2,1)} %bitcast.2, ...), custom_call_target="tpu_custom_call" | custom-call | tf_op jit(solution)/shard_map/first_part/pallas_call | solution.py:701
  281.9 97.1 %second_part.1 = (bf16[32,2816]{1,0:T(8,128)(2,1)}, bf16[32,2816]{1,0:T(8,128)(2,1)}, bf16[88,1024]{1,0:T(8,128)(2,1)}, f32[8,128]{1,0:T(8,128)}, bf16[11,4,4,2,...) custom-call(f32[8,128]{1,0:T(8,128)} %get-tuple-element.23.refs_0_, ...), custom_call_target="tpu_custom_call" | custom-call | tf_op jit(solution)/shard_map/second_part/pallas_call | solution.py:772
  379.0 5.9 %adamw.1 = (bf16[2,32,2816]{2,1,0:T(8,128)(2,1)}, bf16[2,32,2816]{2,1,0:T(8,128)(2,1)}, bf16[2,88,1024]{2,1,0:T(8,128)(2,1)}, f32[2,32,2816]{2,1,0:T(8,128)}, f3...) custom-call(f32[8,128]{1,0:T(8,128)} %get-tuple-element.30.squares_r, ...), custom_call_target="tpu_custom_call" | custom-call | tf_op jit(solution)/shard_map/adamw/pallas_call | solution.py:805
